TPU v7x, 32 devices: a whole 2x2x4 slice. The times are simulated.
32 devices in a mesh: col: 4 (over z), row: 8 (over y, x, core).
Axes of the slice: x: 2, y: 2, z: 4, core: 2. Of those that a mesh axis runs over, the one named last changes fastest.
Arguments:
- vel_u: float32 [31, 512, 2048], P(None, 'row', 'col')
- vel_v: float32 [31, 512, 2048], P(None, 'row', 'col')
- temperature: float32 [31, 512, 2048], P(None, 'row', 'col')
- salinity: float32 [31, 512, 2048], P(None, 'row', 'col')
- sea_level: float32 [512, 2048], P('row', 'col')
- trans_u: float32 [512, 2048], P('row', 'col')
- trans_v: float32 [512, 2048], P('row', 'col')
- bathymetry: float32 [512, 2048], P('row', 'col')
- kmt_levels: int32 [512, 2048], P('row', 'col')
- tide_force: float32 [30, 2], replicated
Outputs:
- output 1: float32 [512, 2048], P('row', 'col')
- output 2: float32 [512, 2048], P('row', 'col')
- output 3: float32 [512, 2048], P('row', 'col')
- output 4: float32 [31, 512, 2048], P(None, 'row', 'col')
- output 5: float32 [31, 512, 2048], P(None, 'row', 'col')
- output 6: float32 [31, 512, 2048], P(None, 'row', 'col')
- output 7: float32 [31, 512, 2048], P(None, 'row', 'col')
All inputs are finite; a program needn't handle non-finite values.
Results may differ from a plain program's by a relative error of at most 0.001.
Values sent between devices are 32-bit elements.
A program may use at most 1 GiB of HBM per device.

v0:
```python
import jax
import jax.numpy as jnp
from jax import lax
from jax.sharding import PartitionSpec as P

GRAVITY = 1.0
GRID_DX = 1.0
TIME_STEP = 4.0
ALPHA_T = 0.02
BETA_S = 0.015
T_REF = 1.0
S_REF = 1.0
VISC_KV = 0.001
DIFF_KT = 0.0005


def level_mask(count, n_levels):
    levels = jnp.arange(n_levels, dtype=jnp.int32)[:, None, None]
    return (levels < count[None]).astype(jnp.float32)


def interface_coef(count, thick, kappa, n_levels):
    levels = jnp.arange(n_levels - 1, dtype=jnp.int32)[:, None, None]
    active = (levels + 1 < count[None]).astype(jnp.float32)
    safe = jnp.where(count > 0, thick, 1.0)
    return active * (TIME_STEP * kappa / (safe * safe))[None]


def column_solve(source, couple):
    edge = jnp.zeros_like(source[:1])
    upper = jnp.concatenate([couple, edge], axis=0)
    lower = jnp.concatenate([edge, couple], axis=0)
    diag = 1.0 + upper + lower

    def forward(carry, slab):
        gain_prev, part_prev = carry
        lower_k, diag_k, upper_k, source_k = slab
        pivot = diag_k - lower_k * gain_prev
        gain = upper_k / pivot
        part = (source_k + lower_k * part_prev) / pivot
        return (gain, part), (gain, part)

    start = (jnp.zeros_like(source[0]), jnp.zeros_like(source[0]))
    _, (gains, parts) = lax.scan(forward, start, (lower, diag, upper, source))

    def backward(below, slab):
        gain, part = slab
        here = part + gain * below
        return here, here

    _, profile = lax.scan(backward, jnp.zeros_like(source[0]), (gains, parts), reverse=True)
    return profile


def geometry(kmt_ext, depth_ext):
    kmt_cell = kmt_ext[1:-1, 1:-1]
    thick_ext = depth_ext / jnp.maximum(kmt_ext, 1).astype(jnp.float32)
    thick_cell = thick_ext[1:-1, 1:-1]
    return {"k_cell": kmt_cell, "k_u": jnp.minimum(kmt_cell, kmt_ext[1:-1, 2:]), "k_v": jnp.minimum(kmt_cell, kmt_ext[2:, 1:-1]), "dz_cell": thick_cell, "dz_u": 0.5 * (thick_cell + thick_ext[1:-1, 2:]), "dz_v": 0.5 * (thick_cell + thick_ext[2:, 1:-1])}


def surface_fields(layout):
    k_faces = jnp.stack([layout["k_u"], layout["k_v"]])
    face_depth = k_faces.astype(jnp.float32) * jnp.stack([layout["dz_u"], layout["dz_v"]])
    face_wet = (k_faces > 0).astype(jnp.float32)
    wet_cell = (layout["k_cell"] > 0).astype(jnp.float32)
    return face_depth, face_wet, wet_cell


def momentum_tend(u_ext, v_ext, p_ext):
    cen_u = 0.5 * (u_ext[:, 1:-1, :-1] + u_ext[:, 1:-1, 1:])
    corner_v = 0.5 * (v_ext[:, :-1, 1:-1] + v_ext[:, :-1, 2:])
    corner_u = 0.5 * (u_ext[:, :-1, 1:-1] + u_ext[:, 1:, 1:-1])
    flux_uu = cen_u * cen_u
    flux_vu = corner_v * corner_u
    tend_u = -(flux_uu[:, :, 1:] - flux_uu[:, :, :-1] + flux_vu[:, 1:, :] - flux_vu[:, :-1, :] + p_ext[:, 1:-1, 2:] - p_ext[:, 1:-1, 1:-1]) / GRID_DX
    cen_v = 0.5 * (v_ext[:, :-1, 1:-1] + v_ext[:, 1:, 1:-1])
    side_u = 0.5 * (u_ext[:, 1:-1, :-1] + u_ext[:, 2:, :-1])
    side_v = 0.5 * (v_ext[:, 1:-1, :-1] + v_ext[:, 1:-1, 1:])
    flux_vv = cen_v * cen_v
    flux_uv = side_u * side_v
    tend_v = -(flux_vv[:, 1:, :] - flux_vv[:, :-1, :] + flux_uv[:, :, 1:] - flux_uv[:, :, :-1] + p_ext[:, 2:, 1:-1] - p_ext[:, 1:-1, 1:-1]) / GRID_DX
    return tend_u, tend_v


def baroclinic_predict(vel_u, vel_v, value_a11, salinity, layout, halo_fn):
    n_levels = vel_u.shape[0]
    mask_c = level_mask(layout["k_cell"], n_levels)
    mask_u = level_mask(layout["k_u"], n_levels)
    mask_v = level_mask(layout["k_v"], n_levels)
    vel_um = vel_u * mask_u
    vel_vm = vel_v * mask_v
    density = mask_c * (BETA_S * (salinity - S_REF) - ALPHA_T * (value_a11 - T_REF))
    pressure = GRAVITY * layout["dz_cell"] * (jnp.cumsum(density, axis=0) - 0.5 * density)
    cell_coef = interface_coef(layout["k_cell"], layout["dz_cell"], DIFF_KT, n_levels)
    temp_mix = column_solve(value_a11 * mask_c, cell_coef)
    salt_mix = column_solve(salinity * mask_c, cell_coef)
    edges = halo_fn(jnp.stack([vel_um, vel_vm, pressure, temp_mix, salt_mix]))
    tend_u, tend_v = momentum_tend(edges[0], edges[1], edges[2])
    u_star = column_solve(mask_u * (vel_um + TIME_STEP * tend_u), interface_coef(layout["k_u"], layout["dz_u"], VISC_KV, n_levels))
    v_star = column_solve(mask_v * (vel_vm + TIME_STEP * tend_v), interface_coef(layout["k_v"], layout["dz_v"], VISC_KV, n_levels))
    forcing = jnp.stack([jnp.sum(layout["dz_u"] * (u_star - vel_um), axis=0), jnp.sum(layout["dz_v"] * (v_star - vel_vm), axis=0)]) / TIME_STEP
    return u_star, v_star, forcing, edges[3:], (mask_c, mask_u, mask_v)


def barotropic(eta_start, trans_start, face_depth, face_wet, wet_cell, forcing, tide_force, halo_fn):
    n_sub = tide_force.shape[0]
    dt_sub = TIME_STEP / n_sub
    weight_norm = 6.0 / (n_sub * (n_sub + 1) * (n_sub + 2))

    def substep(step, carry):
        eta_now, trans_now, trans_avg = carry
        trans_ext = halo_fn(trans_now)
        divergence = (trans_now[0] - trans_ext[0, 1:-1, :-2] + trans_now[1] - trans_ext[1, :-2, 1:-1]) / GRID_DX
        eta_next = wet_cell * (eta_now - dt_sub * divergence)
        eta_ext = halo_fn(eta_next)
        slope = jnp.stack([eta_ext[1:-1, 2:] - eta_next, eta_ext[2:, 1:-1] - eta_next]) / GRID_DX
        tide_now = lax.dynamic_index_in_dim(tide_force, step, 0, keepdims=False)
        trans_next = face_wet * (trans_now + dt_sub * (face_depth * (tide_now[:, None, None] - GRAVITY * slope) + forcing))
        weight = weight_norm * ((step + 1) * (n_sub - step)).astype(jnp.float32)
        return eta_next, trans_next, trans_avg + weight * trans_next

    return lax.fori_loop(0, n_sub, substep, (eta_start, trans_start, jnp.zeros_like(trans_start)))


def correct_velocity(star, dz_face, depth_face, mean_trans, mask):
    safe = jnp.where(depth_face > 0, depth_face, 1.0)
    return mask * (star + ((mean_trans - jnp.sum(dz_face * star, axis=0)) / safe)[None])


def advect_tracers(tracer_ext, flow_ext, mask_c):
    flux_x = flow_ext[0, :, 1:-1, :-1] * (0.5 * (tracer_ext[..., 1:-1, :-1] + tracer_ext[..., 1:-1, 1:]))
    flux_y = flow_ext[1, :, :-1, 1:-1] * (0.5 * (tracer_ext[..., :-1, 1:-1] + tracer_ext[..., 1:, 1:-1]))
    divergence = (flux_x[..., 1:] - flux_x[..., :-1] + flux_y[..., 1:, :] - flux_y[..., :-1, :]) / GRID_DX
    return mask_c * (tracer_ext[..., 1:-1, 1:-1] - TIME_STEP * divergence)


def baroclinic_finish(u_star, v_star, trans_avg, face_depth, layout, tracer_ext, masks, halo_fn):
    mask_c, mask_u, mask_v = masks
    vel_uc = correct_velocity(u_star, layout["dz_u"], face_depth[0], trans_avg[0], mask_u)
    vel_vc = correct_velocity(v_star, layout["dz_v"], face_depth[1], trans_avg[1], mask_v)
    flows = halo_fn(jnp.stack([vel_uc, vel_vc]))
    tracers = advect_tracers(tracer_ext, flows, mask_c)
    return vel_uc, vel_vc, tracers[0], tracers[1]


def ocean_step(vel_u, vel_v, value_a11, salinity, sea_level, trans_u, trans_v, bathymetry, kmt_levels, tide_force, halo_fn):
    layout = geometry(halo_fn(kmt_levels), halo_fn(bathymetry))
    u_star, v_star, forcing, tracer_ext, masks = baroclinic_predict(vel_u, vel_v, value_a11, salinity, layout, halo_fn)
    face_depth, face_wet, wet_cell = surface_fields(layout)
    eta_new, trans_new, trans_avg = barotropic(wet_cell * sea_level, face_wet * jnp.stack([trans_u, trans_v]), face_depth, face_wet, wet_cell, forcing, tide_force, halo_fn)
    vel_uc, vel_vc, temp_new, salt_new = baroclinic_finish(u_star, v_star, trans_avg, face_depth, layout, tracer_ext, masks, halo_fn)
    return eta_new, trans_new[0], trans_new[1], vel_uc, vel_vc, temp_new, salt_new


def solution(mesh):
    n_cols = mesh.shape["col"]
    n_rows = mesh.shape["row"]
    east_perm = [(member, (member - 1) % n_cols) for member in range(n_cols)]
    west_perm = [(member, (member + 1) % n_cols) for member in range(n_cols)]
    north_perm = [(member, member - 1) for member in range(1, n_rows)]
    south_perm = [(member, member + 1) for member in range(n_rows - 1)]

    def halo_swap(field):
        from_east = lax.ppermute(field[..., :1], "col", east_perm)
        from_west = lax.ppermute(field[..., -1:], "col", west_perm)
        wide = jnp.concatenate([from_west, field, from_east], axis=-1)
        from_north = lax.ppermute(wide[..., :1, :], "row", north_perm)
        from_south = lax.ppermute(wide[..., -1:, :], "row", south_perm)
        return jnp.concatenate([from_south, wide, from_north], axis=-2)

    def local_step(vel_u, vel_v, value_a11, salinity, sea_level, trans_u, trans_v, bathymetry, kmt_levels, tide_force):
        return ocean_step(vel_u, vel_v, value_a11, salinity, sea_level, trans_u, trans_v, bathymetry, kmt_levels, tide_force, halo_swap)

    spec_cube = P(None, "row", "col")
    spec_plane = P("row", "col")
    return jax.shard_map(local_step, mesh=mesh, in_specs=(spec_cube, spec_cube, spec_cube, spec_cube, spec_plane, spec_plane, spec_plane, spec_plane, spec_plane, P(None, None)), out_specs=(spec_plane, spec_plane, spec_plane, spec_cube, spec_cube, spec_cube, spec_cube), check_vma=False)
```

profile of v0, /device:TPU:0, one launch (start us, length us, event | category | flops | bytes accessed | tf_op | source)
XLA Modules:
  0.0 1440.6 jit_solution(9176421462549483770)
XLA Ops:
  1.5 5.1 collective-permute-start.6
  11.3 8.5 fusion.61
  33.3 4.4 compare_select_fusion.2
  37.6 5.4 fusion.99
  48.0 59.3 %while.156 = (s32[]{:T(128)}, f32[64,512]{1,0:T(8,128)S(1)}, f32[64,512]{1,0:T(8,128)S(1)}, f32[31,64,512]{2,1,0:T(8,128)}, f32[31,64,512]{2,1,0:T(8,128)}, /*in...) while((s32[]{:T(128)}, f32[64,512]{1,0:T(8,128)S(1)}, ...), condition=%wide.region_6.7_spmd.clone, body=%wide.region_5.6_spmd.clone.sunk | while | flops 262147 | bytes 1311351 | solution.py:44
  109.8 53.4 %while.157 = (s32[]{:T(128)}, f32[64,512]{1,0:T(8,128)S(1)}, f32[31,64,512]{2,1,0:T(8,128)}, f32[31,64,512]{2,1,0:T(8,128)}, f32[31,64,512]{2,1,0:T(8,128)}, /*index=5*/s32[]{:T(128)}, s32[]{:T(128)}, s32[]{:T(128)}) while((s32[]{:T(128)}, f32[64,512]{1,0:T(8,128)S(1)}, f32[31,64,512]{2,1,0:T(8,128)}, f32[31,64,512]{2,1,0:T(8,128)}, ...), condition=%wide.region_8.9_spmd.clone, body=%wide.region_7.8_spmd.clone.sunk | while | flops 98308 | bytes 655471 | solution.py:51
  168.1 59.3 %while.154 = (s32[]{:T(128)}, f32[64,512]{1,0:T(8,128)S(1)}, f32[64,512]{1,0:T(8,128)S(1)}, f32[31,64,512]{2,1,0:T(8,128)}, f32[31,64,512]{2,1,0:T(8,128)}, /*in...) while((s32[]{:T(128)}, f32[64,512]{1,0:T(8,128)S(1)}, ...), condition=%wide.region_2.3_spmd.clone, body=%wide.region_1.2_spmd.clone.sunk | while | flops 262147 | bytes 1311351 | solution.py:44
  229.9 53.4 %while.155 = (s32[]{:T(128)}, f32[64,512]{1,0:T(8,128)S(1)}, f32[31,64,512]{2,1,0:T(8,128)}, f32[31,64,512]{2,1,0:T(8,128)}, f32[31,64,512]{2,1,0:T(8,128)}, /*index=5*/s32[]{:T(128)}, s32[]{:T(128)}, s32[]{:T(128)}) while((s32[]{:T(128)}, f32[64,512]{1,0:T(8,128)S(1)}, f32[31,64,512]{2,1,0:T(8,128)}, f32[31,64,512]{2,1,0:T(8,128)}, ...), condition=%wide.region_4.5_spmd.clone, body=%wide.region_3.4_spmd.clone.sunk | while | flops 98308 | bytes 655471 | solution.py:51
  283.3 5.0 bitcast_dynamic-update-slice_fusion.14
  291.0 10.3 bitcast_dynamic-update-slice_fusion.12
  301.3 4.9 constant_dynamic-update-slice_fusion.1
  308.7 9.4 fusion.97
  325.5 3.9 collective-permute-start.15
  329.3 8.9 fusion.98
  338.2 5.4 fusion.100
  350.2 5.3 pad_maximum_fusion.34
  355.4 4.0 collective-permute-start.16
  363.0 15.7 %maximum_bitcast_fusion.1 = (f32[31,66,514]{2,1,0:T(8,128)S(1)}, f32[31,66,514]{2,1,0:T(8,128)}, f32[31,66,514]{2,1,0:T(8,128)}) fusion(f32[5,31,1,514]{3,2,1,0:T(1,128)S(1)} %collective-permute-done.17, f32[5,31,1,514]{3,2,1,0:T(1,128)S(1)} %collective-permute-done.16, f32[5,31,64,1]{3,2,1,0:T(8,128)} %copy.21, ...), kind=kLoop, calls=%fused_computation.99 | loop fusion | flops 12619728 | bytes 33652608 | tf_op jit(solution)/shard_map/squeeze | solution.py:99
  378.8 11.6 fusion.42
  390.4 15.1 %fusion.48 = (f32[31,65,512]{2,1,0:T(8,128)}, f32[31,65,512]{2,1,0:T(8,128)}) fusion(f32[31,66,514]{2,1,0:T(8,128)S(1)} %get-tuple-element.1206, f32[31,66,514]{2,1,0:T(8,128)} %get-tuple-element.1207), kind=kLoop, calls=%fused_computation.123 | loop fusion | flops 8253440 | bytes 28887040 | tf_op jit(solution)/shard_map/mul | solution.py:75
  405.5 24.2 %fusion.59 = (f32[31,64,512]{2,1,0:T(8,128)}, f32[31,64,512]{2,1,0:T(8,128)}) fusion(f32[31,66,514]{2,1,0:T(8,128)} %get-tuple-element.1208, f32[31,65,512]{2,1,0:T(8,128)} %get-tuple-element.1221, f32[31,64,513]{2,1,0:T(8,128)} %get-tuple-element.1219, f32[31,64,512]{2,1,0:T(8,128)S(1)} %copy-done.6, s32[64,512]{1,0:T(8,128)S(1)} %get-tuple-element.1186, ...), kind=kLoop, calls=%fused_computation.142 | loop fusion | flops 22347776 | bytes 61210624 | tf_op jit(solution)/shard_map/mul | solution.py:100
  434.7 59.3 %while.158 = (s32[]{:T(128)}, f32[64,512]{1,0:T(8,128)S(1)}, f32[64,512]{1,0:T(8,128)S(1)}, f32[31,64,512]{2,1,0:T(8,128)}, f32[31,64,512]{2,1,0:T(8,128)}, /*in...) while((s32[]{:T(128)}, f32[64,512]{1,0:T(8,128)S(1)}, ...), condition=%wide.region_10.11_spmd.clone, body=%wide.region_9.10_spmd.clone.sunk | while | flops 262147 | bytes 1311351 | solution.py:44
  496.5 53.4 %while.159 = (s32[]{:T(128)}, f32[64,512]{1,0:T(8,128)S(1)}, f32[31,64,512]{2,1,0:T(8,128)}, f32[31,64,512]{2,1,0:T(8,128)}, f32[31,64,512]{2,1,0:T(8,128)}, /*index=5*/s32[]{:T(128)}, s32[]{:T(128)}, s32[]{:T(128)}) while((s32[]{:T(128)}, f32[64,512]{1,0:T(8,128)S(1)}, f32[31,64,512]{2,1,0:T(8,128)}, ...), condition=%wide.region_12.13_spmd.clone, body=%wide.region_11.12_spmd.clone.sunk | while | flops 98308 | bytes 655471 | solution.py:51
  549.9 4.5 multiply_reduce_fusion.1
  559.4 59.3 %while.160 = (s32[]{:T(128)}, f32[64,512]{1,0:T(8,128)S(1)}, f32[64,512]{1,0:T(8,128)S(1)}, f32[31,64,512]{2,1,0:T(8,128)}, f32[31,64,512]{2,1,0:T(8,128)}, /*in...) while((s32[]{:T(128)}, f32[64,512]{1,0:T(8,128)S(1)}, ...), condition=%wide.region_15.16_spmd.clone, body=%wide.region_14.15_spmd.clone.sunk | while | flops 262147 | bytes 1311351 | solution.py:44
  621.1 53.6 %while.161 = (s32[]{:T(128)}, f32[64,512]{1,0:T(8,128)S(1)}, f32[31,64,512]{2,1,0:T(8,128)}, f32[31,64,512]{2,1,0:T(8,128)}, f32[31,64,512]{2,1,0:T(8,128)}, /*index=5*/s32[]{:T(128)}, s32[]{:T(128)}, s32[]{:T(128)}) while((s32[]{:T(128)}, f32[64,512]{1,0:T(8,128)S(1)}, f32[31,64,512]{2,1,0:T(8,128)}, ...), condition=%wide.region_17.18_spmd.clone, body=%wide.region_16.17_spmd.clone.sunk | while | flops 98308 | bytes 655471 | solution.py:51
  674.7 4.5 multiply_reduce_fusion
  679.3 668.7 %while.162 = (s32[]{:T(128)}, f32[64,512]{1,0:T(8,128)S(1)}, f32[2,64,512]{2,1,0:T(8,128)S(1)}, f32[2,64,512]{2,1,0:T(8,128)S(1)}, f32[64,512]{1,0:T(8,128)S(1)}...) while((s32[]{:T(128)}, f32[64,512]{1,0:T(8,128)S(1)}, ...), condition=%wide.region_20.21_spmd.clone, body=%wide.region_19.20_spmd.clone.sunk | while | flops 1182739 | bytes 3981899 | solution.py:123
  687.3 8.9 collective-permute-start.2
  713.5 4.6 collective-permute-start.2
  777.3 4.9 collective-permute-start.2
  799.3 5.1 collective-permute-start.2
  821.5 5.1 collective-permute-start.2
  843.7 5.1 collective-permute-start.2
  865.9 5.1 collective-permute-start.2
  888.1 5.1 collective-permute-start.2
  910.3 5.1 collective-permute-start.2
  932.5 5.1 collective-permute-start.2
  954.7 5.1 collective-permute-start.2
  976.9 5.1 collective-permute-start.2
  999.1 5.1 collective-permute-start.2
  1021.3 5.1 collective-permute-start.2
  1043.5 5.1 collective-permute-start.2
  1065.7 5.1 collective-permute-start.2
  1087.9 5.1 collective-permute-start.2
  1110.1 5.1 collective-permute-start.2
  1132.3 5.1 collective-permute-start.2
  1154.5 5.1 collective-permute-start.2
  1176.7 5.1 collective-permute-start.2
  1198.9 5.1 collective-permute-start.2
  1221.1 5.1 collective-permute-start.2
  1243.3 5.1 collective-permute-start.2
  1265.5 5.1 collective-permute-start.2
  1287.7 5.1 collective-permute-start.2
  1309.9 5.1 collective-permute-start.2
  1332.1 5.1 collective-permute-start.2
  1348.0 4.5 add_select_fusion
  1359.5 4.0 collective-permute-start.19
  1365.1 5.9 fusion.37
  1375.0 5.5 collective-permute-start.20
  1380.5 13.8 fusion.29
  1397.1 13.1 fusion.31
  1410.2 21.5 %fusion.34 = f32[2,31,64,512]{3,2,1,0:T(8,128)} fusion(f32[2,31,65,512]{3,2,1,0:T(8,128)} %fusion.31, f32[2,31,64,513]{3,2,1,0:T(8,128)} %fusion.29, f32[1,31,64,512]{3,2,1,0:T(8,128)} %bitcast.268, f32[1,31,64,512]{3,2,1,0:T(8,128)} %bitcast.269, f32[31,64,512]{2,1,0:T(8,128)} %fusion.60), kind=kLoop, calls=%fused_computation.90 | loop fusion | flops 14221312 | bytes 52822016 | tf_op jit(solution)/shard_map/mul | solution.py:135
  1431.8 8.4 slice_bitcast_fusion
  (942 shorter events, 1056.9 us)
Async XLA Ops:
  1.5 20.8 %collective-permute-start.6 = (s32[64,1]{1,0:T(8,128)S(1)}, s32[64,1]{1,0:T(8,128)S(1)}, u32[]{:S(2)}, u32[]{:S(2)}) collective-permute-start(s32[64,1]{1,0:T(8,128)S(1)} %get-tuple-element.1249), channel_id=1, source_target_pairs={{0,24},{8,0},{16,8},{24,16},{1,25},{9,1},{17,9},{25,17},{2,26},{10... | collective-permute-start | bytes 776 | tf_op jit(solution)/shard_map/ppermute | solution.py:165
  6.6 15.6 %collective-permute-start.7 = (s32[64,1]{1,0:T(8,128)S(1)}, s32[64,1]{1,0:T(8,128)S(1)}, u32[]{:S(2)}, u32[]{:S(2)}) collective-permute-start(s32[64,1]{1,0:T(8,128)S(1)} %get-tuple-element.1248), channel_id=1, source_target_pairs={{0,8},{8,16},{16,24},{24,0},{1,9},{9,17},{17,25},{25,1},{2,10},{10... | collective-permute-start | bytes 776 | tf_op jit(solution)/shard_map/ppermute | solution.py:166
  7.5 19.2 %collective-permute-start.10 = (f32[64,1]{1,0:T(8,128)S(1)}, f32[64,1]{1,0:T(8,128)S(1)}, u32[]{:S(2)}, u32[]{:S(2)}) collective-permute-start(f32[64,1]{1,0:T(8,128)S(1)} %get-tuple-element.1251), channel_id=1, source_target_pairs={{0,24},{8,0},{16,8},{24,16},{1,25},{9,1},{17,9},{25,17},{2,26},{10... | collective-permute-start | bytes 776 | tf_op jit(solution)/shard_map/ppermute | solution.py:165
  11.3 15.4 %collective-permute-start.9 = (f32[64,1]{1,0:T(8,128)S(1)}, f32[64,1]{1,0:T(8,128)S(1)}, u32[]{:S(2)}, u32[]{:S(2)}) collective-permute-start(f32[64,1]{1,0:T(8,128)S(1)} %get-tuple-element.1250), channel_id=1, source_target_pairs={{0,8},{8,16},{16,24},{24,0},{1,9},{9,17},{17,25},{25,1},{2,10},{10... | collective-permute-start | bytes 776 | tf_op jit(solution)/shard_map/ppermute | solution.py:166
  22.3 9.0 collective-permute-start.8
  23.6 7.7 collective-permute-start.13
  321.5 22.2 %collective-permute-start.14 = (f32[5,31,64,1]{2,3,1,0:T(1,128)S(1)}, f32[5,31,64,1]{2,3,1,0:T(1,128)S(1)}, u32[]{:S(2)}, u32[]{:S(2)}) collective-permute-start(f32[5,31,64,1]{2,3,1,0:T(1,128)S(1)} %copy.18), channel_id=1, source_target_pairs={{0,8},{8,16},{16,24},{24,0},{1,9},{9,17},{17,25},{25,1},{2,10},{10... | collective-permute-start | bytes 119048 | tf_op jit(solution)/shard_map/ppermute | solution.py:166
  325.5 21.4 %collective-permute-start.15 = (f32[5,31,64,1]{2,3,1,0:T(1,128)S(1)}, f32[5,31,64,1]{2,3,1,0:T(1,128)S(1)}, u32[]{:S(2)}, u32[]{:S(2)}) collective-permute-start(f32[5,31,64,1]{2,3,1,0:T(1,128)S(1)} %copy.19), channel_id=1, source_target_pairs={{0,24},{8,0},{16,8},{24,16},{1,25},{9,1},{17,9},{25,17},{2,26},{10... | collective-permute-start | bytes 119048 | tf_op jit(solution)/shard_map/ppermute | solution.py:165
  681.2 6.1 collective-permute-start.1
  687.3 9.7 collective-permute-start.2
  707.1 6.4 collective-permute-start.1
  729.1 6.1 collective-permute-start.1
  740.4 6.1 collective-permute-start.4
  750.1 6.4 collective-permute-start.1
  771.1 6.1 collective-permute-start.1
  783.5 6.0 collective-permute-start.4
  793.1 6.1 collective-permute-start.1
  815.3 6.1 collective-permute-start.1
  827.9 6.0 collective-permute-start.4
  837.5 6.1 collective-permute-start.1
  850.1 6.0 collective-permute-start.4
  859.7 6.1 collective-permute-start.1
  872.3 6.0 collective-permute-start.4
  881.9 6.1 collective-permute-start.1
  894.5 6.0 collective-permute-start.4
  904.1 6.1 collective-permute-start.1
  916.7 6.0 collective-permute-start.4
  926.3 6.1 collective-permute-start.1
  938.9 6.0 collective-permute-start.4
  948.5 6.1 collective-permute-start.1
  961.1 6.0 collective-permute-start.4
  970.7 6.1 collective-permute-start.1
  983.3 6.0 collective-permute-start.4
  992.9 6.1 collective-permute-start.1
  1005.5 6.0 collective-permute-start.4
  1015.1 6.1 collective-permute-start.1
  1027.7 6.0 collective-permute-start.4
  1037.3 6.1 collective-permute-start.1
  1049.9 6.0 collective-permute-start.4
  1059.5 6.1 collective-permute-start.1
  1072.1 6.0 collective-permute-start.4
  1081.7 6.1 collective-permute-start.1
  1094.3 6.0 collective-permute-start.4
  1103.9 6.1 collective-permute-start.1
  1116.5 6.0 collective-permute-start.4
  1126.1 6.1 collective-permute-start.1
  1138.7 6.0 collective-permute-start.4
  1148.3 6.1 collective-permute-start.1
  1160.9 6.0 collective-permute-start.4
  1170.5 6.1 collective-permute-start.1
  1183.1 6.0 collective-permute-start.4
  1192.7 6.1 collective-permute-start.1
  1205.3 6.0 collective-permute-start.4
  1214.9 6.1 collective-permute-start.1
  1237.1 6.1 collective-permute-start.1
  1249.7 6.0 collective-permute-start.4
  1259.3 6.1 collective-permute-start.1
  1271.9 6.0 collective-permute-start.4
  1281.5 6.1 collective-permute-start.1
  1294.1 6.0 collective-permute-start.4
  1303.7 6.1 collective-permute-start.1
  1325.9 6.1 collective-permute-start.1
  1359.5 11.5 collective-permute-start.19
  1375.0 19.3 %collective-permute-start.20 = (f32[2,31,1,514]{3,2,1,0:T(1,128)S(1)}, f32[2,31,1,514]{3,2,1,0:T(1,128)S(1)}, u32[]{:S(2)}, u32[]{:S(2)}) collective-permute-start(f32[2,31,1,514]{3,2,1,0:T(1,128)S(1)} %pad_maximum_fusion.35), channel_id=1, source_target_pairs={{0,1},{1,2},{2,3},{3,4},{4,5},{5,6},{6,7},{8,9},{9,10},{10,11},{11... | collective-permute-start | bytes 382424 | tf_op jit(solution)/shard_map/ppermute | solution.py:169
  (151 other events, 822.1 us)
where the time goes:
time: 1460 us; the launch traced here: 1440 us
  other arithmetic  671 us (46%)
  starting transfers between devices  352 us (24%)
  waiting for transfers between devices  331 us (23%)
  local copies, waits for them, and re-layouts  82.9 us (6%)
    dynamic_update_slice x248, other arithmetic, column_solve(): _, (gains, parts) = lax.scan(forward, start, (lower, diag, upper, source))  451 us
    ppermute x34, starting transfers between devices, halo_swap(): from_south = lax.ppermute(wide[..., -1:, :], 'row', south_perm)  170 us
    ppermute x64, waiting for transfers between devices, halo_swap(): from_east = lax.ppermute(field[..., :1], 'col', east_perm)  126 us
    ppermute x64, waiting for transfers between devices, halo_swap(): from_west = lax.ppermute(field[..., -1:], 'col', west_perm)  125 us
    ppermute x64, starting transfers between devices, halo_swap(): from_west = lax.ppermute(field[..., -1:], 'col', west_perm)  112 us
    ppermute x33, waiting for transfers between devices, halo_swap(): from_north = lax.ppermute(wide[..., :1, :], 'row', north_perm)  55.4 us
    ppermute x33, starting transfers between devices, halo_swap(): from_north = lax.ppermute(wide[..., :1, :], 'row', north_perm)  42.5 us
    another operation x12, local copies, waits for them, and re-layouts  29.9 us
  transfers between devices with their start and end apart: 195, of which 183 were waited for; matrix products, arithmetic and copies ran while one was open for 4% of the time, Pallas kernels for 0%

commit v1 on v0

v1 whole, which is shorter than its diff:
```python
import jax
import jax.numpy as jnp
from jax import lax
from jax.experimental import pallas as pl
from jax.experimental.pallas import tpu as pltpu
from jax.sharding import PartitionSpec as P

GRAVITY = 1.0
TIME_STEP = 4.0
ALPHA_T = 0.02
BETA_S = 0.015
T_REF = 1.0
S_REF = 1.0
VISC_KV = 0.001
DIFF_KT = 0.0005

LANES = 128
HALO = 32
PAD = 8
F32 = jnp.float32
NORTH, SOUTH, EAST, WEST = (1, 0), (-1, 0), (0, 1), (0, -1)
NORTH_EAST, NORTH_WEST, SOUTH_EAST, SOUTH_WEST = (1, 1), (1, -1), (-1, 1), (-1, -1)
COMPASS = (NORTH, SOUTH, EAST, WEST, NORTH_EAST, NORTH_WEST, SOUTH_EAST, SOUTH_WEST)
SLOT = 32
BLOCK = 16
CROSS_ROWS = 8
FLOW_ROWS = 8
SOLVE_ROWS = 32
SUB_ROWS = 16
BACK_ROWS = 8
MIB = 2**20


def kernels(mesh, levels, rows, cols, n_sub):
    n_cols, n_rows = mesh.shape["col"], mesh.shape["row"]
    tiles = cols // LANES
    ring = tiles + 1
    halo_tile = tiles
    ext_rows = rows + 2 * PAD
    flat_rows = rows + 2 * HALO + 2 * PAD
    core = PAD + HALO
    top = core + rows
    body_rows = pl.ds(PAD, rows)
    own = pl.ds(core, rows)
    dt_sub = TIME_STEP / n_sub
    weight_norm = 6.0 / (n_sub * (n_sub + 1) * (n_sub + 2))

    def lane_iota(n):
        return lax.broadcasted_iota(jnp.int32, (n, LANES), 1)

    def roll(x, shift):
        return pltpu.roll(x, shift, 1)

    def east(parts):
        last = lane_iota(parts[0].shape[0]) == LANES - 1
        moved = [roll(x, LANES - 1) for x in parts]
        return [jnp.where(last, moved[(c + 1) % ring], moved[c]) for c in range(ring)]

    def west(parts):
        first = lane_iota(parts[0].shape[0]) == 0
        moved = [roll(x, 1) for x in parts]
        return [jnp.where(first, moved[(c - 1) % ring], moved[c]) for c in range(ring)]

    def split(ref):
        return [ref.at[f] for f in range(ref.shape[0])]

    def scaled(factor, x):
        return x if factor == 1.0 else factor * x

    def blank():
        return jnp.zeros((rows, LANES), F32)

    def neighbour(way):
        d_row, d_col = way
        row = lax.rem(lax.axis_index("row") + (d_row + n_rows), n_rows)
        col = lax.rem(lax.axis_index("col") + (d_col + n_cols), n_cols)
        return {"row": row, "col": col}

    def remote(sems, *routes):
        sent, arrived = split(sems)
        return [
            pltpu.make_async_remote_copy(
                src_ref=src,
                dst_ref=dst,
                send_sem=sent.at[index],
                recv_sem=arrived.at[index],
                device_id=neighbour(way),
                device_id_type=pl.DeviceIdType.MESH,
            )
            for index, (src, dst, way) in enumerate(routes)
        ]

    def start_all(copies):
        for copy in copies:
            copy.start()

    def wait_all(copies):
        for copy in copies:
            copy.wait()

    def rim_pack(maps, pack_east, pack_west):
        slot = lane_iota(rows) // HALO
        last, first = blank(), blank()
        for f, ref in enumerate(maps):
            last = jnp.where(slot == f, roll(ref[tiles - 1, own, :], (HALO * f + HALO) % LANES), last)
            first = jnp.where(slot == f, roll(ref[0, own, :], HALO * f), first)
        pack_east[...] = last
        pack_west[...] = first

    def rim_copies(main, pack_east, pack_west, from_west, from_east, sems):
        inner = pl.ds(0, tiles)
        low, high = pl.ds(core, HALO), pl.ds(top - HALO, HALO)
        p_low, p_all, p_high = pl.ds(0, HALO), pl.ds(0, rows), pl.ds(rows - HALO, HALO)
        d_low, d_all, d_high = pl.ds(0, HALO), pl.ds(HALO, rows), pl.ds(HALO + rows, HALO)
        every = pl.ds(0, main.shape[0])
        return remote(
            sems,
            (main.at[every, inner, high, :], main.at[every, inner, pl.ds(PAD, HALO), :], NORTH),
            (main.at[every, inner, low, :], main.at[every, inner, pl.ds(top, HALO), :], SOUTH),
            (pack_east.at[p_all, :], from_west.at[d_all, :], EAST),
            (pack_west.at[p_all, :], from_east.at[d_all, :], WEST),
            (pack_east.at[p_high, :], from_west.at[d_low, :], NORTH_EAST),
            (pack_west.at[p_high, :], from_east.at[d_low, :], NORTH_WEST),
            (pack_east.at[p_low, :], from_west.at[d_high, :], SOUTH_EAST),
            (pack_west.at[p_low, :], from_east.at[d_high, :], SOUTH_WEST),
        )

    def rim_unpack(maps, from_west, from_east):
        n = rows + 2 * HALO
        easterly = lane_iota(n) < LANES // 2
        for f, ref in enumerate(maps):
            e = roll(from_east[...], (LANES - HALO * f) % LANES)
            w = roll(from_west[...], LANES - HALO - HALO * f)
            ref[halo_tile, pl.ds(PAD, n), :] = jnp.where(easterly, e, w)

    def front(
        u_hbm, v_hbm, t_hbm, s_hbm, eta_hbm, tu_hbm, tv_hbm, depth_hbm, kmt_hbm, tide,
        us, vs, tm, sm, baro_out, corr, counts,
        u, v, p, gain_a, gain_b, cross, kmt_int, geo, thick, baro, force, coef, mean, depth_sum,
        pk_e, pk_w, rim_w, rim_e, first_col, last_col, first_row, last_row,
        col_e, col_w, row_n, row_s, corner_nw, corner_se,
        col_e4, col_w4, row_n4, row_s4, first_col4, last_col4, first_row4, last_row4,
        load_sems, plane_sems, sem1a, sem1b, sem2, sem3, sem4,
    ):
        k_map, depth_map = split(geo)
        eta_map, tu_map, tv_map = split(baro)
        dz_map, dzu_map, dzv_map = split(thick)
        k_out, ku_map, kv_map = split(counts)
        wet_map, hu_map, hv_map = split(coef)
        fu_map, fv_map = split(force)
        mu_map, mv_map = split(mean)
        su_map, sv_map = split(depth_sum)
        pk_e1, pk_e2, pk_e3 = split(pk_e)
        pk_w1, pk_w2, pk_w3 = split(pk_w)
        rim_e1, rim_e2, rim_e3 = split(rim_e)
        rim_w1, rim_w2, rim_w3 = split(rim_w)
        zero = blank()
        lane = lane_iota(rows)

        barrier = pltpu.get_barrier_semaphore()
        for way in COMPASS:
            pl.semaphore_signal(barrier, device_id=neighbour(way), device_id_type=pl.DeviceIdType.MESH)

        def plane_load(sems, src, dst):
            return [
                pltpu.make_async_copy(src.at[:, pl.ds(c * LANES, LANES)], dst(c), sems.at[c]) for c in range(tiles)
            ]

        def cube_load(sems, src, dst):
            return [
                pltpu.make_async_copy(
                    src.at[:, :, pl.ds(c * LANES, LANES)], dst.at[c, :, body_rows, :], sems.at[c]
                )
                for c in range(tiles)
            ]

        sem_k, sem_h, sem_e, sem_tu, sem_tv = split(plane_sems)
        sem_t, sem_s, sem_u, sem_v = split(load_sems)
        geo_load = plane_load(sem_k, kmt_hbm, lambda c: kmt_int.at[c]) + plane_load(
            sem_h, depth_hbm, lambda c: depth_map.at[c, own, :]
        )
        baro_load = (
            plane_load(sem_e, eta_hbm, lambda c: eta_map.at[c, own, :])
            + plane_load(sem_tu, tu_hbm, lambda c: tu_map.at[c, own, :])
            + plane_load(sem_tv, tv_hbm, lambda c: tv_map.at[c, own, :])
        )
        tracer_load = cube_load(sem_t, t_hbm, tm) + cube_load(sem_s, s_hbm, sm)
        flow_load = cube_load(sem_u, u_hbm, u) + cube_load(sem_v, v_hbm, v)
        start_all(geo_load + baro_load + tracer_load + flow_load)

        zero_rows = jnp.zeros((PAD, LANES), F32)
        for ref in (k_map, depth_map, dz_map, eta_map, tu_map, tv_map):
            for c in range(ring):
                ref[c, pl.ds(0, PAD), :] = zero_rows
                ref[c, pl.ds(flat_rows - PAD, PAD), :] = zero_rows
        for ref in (mu_map, mv_map):
            for c in range(ring):
                ref[c] = jnp.zeros((flat_rows, LANES), F32)

        wait_all(geo_load)
        for c in range(tiles):
            k_map[c, own, :] = kmt_int[c].astype(F32)
        rim_pack((k_map, depth_map), pk_e1, pk_w1)
        pl.semaphore_wait(barrier, len(COMPASS))
        ex1a = rim_copies(geo, pk_e1, pk_w1, rim_w1, rim_e1, sem1a)
        start_all(ex1a)
        wait_all(baro_load)
        rim_pack((eta_map, tu_map, tv_map), pk_e2, pk_w2)
        ex1b = rim_copies(baro, pk_e2, pk_w2, rim_w2, rim_e2, sem1b)
        start_all(ex1b)

        wait_all(tracer_load)
        rho_s, rho_t = 0.5 * BETA_S, 0.5 * ALPHA_T
        rho_0 = rho_t * T_REF - rho_s * S_REF

        def pressure_tile(c, _):
            k_cell = k_map[c, own, :]
            scale = (TIME_STEP * GRAVITY) * (depth_map[c, own, :] / jnp.maximum(k_cell, 1.0))

            def level(k, total):
                half = (rho_s * sm[c, k, body_rows, :] - rho_t * tm[c, k, body_rows, :]) + rho_0
                half = jnp.where(k.astype(F32) < k_cell, half, zero)
                middle = total + half
                p[c, k, body_rows, :] = scale * middle
                return middle + half

            lax.fori_loop(0, levels, level, zero)
            return _

        lax.fori_loop(0, tiles, pressure_tile, 0)

        def tracer_tile(c, _):
            k_cell = k_map[c, own, :]
            dz = depth_map[c, own, :] / jnp.maximum(k_cell, 1.0)
            safe = jnp.where(k_cell > 0, dz, 1.0)
            couple = (TIME_STEP * DIFF_KT) / (safe * safe)

            def down(k, carry):
                lower, keep, part_t, part_s = carry
                kf = k.astype(F32)
                wet = kf < k_cell
                upper = jnp.where(kf + 1.0 < k_cell, couple, zero)
                turn = 1.0 + lower * keep
                inv = 1.0 / (turn + upper)
                gain_a[k] = upper * inv
                part_t = (jnp.where(wet, tm[c, k, body_rows, :], zero) + lower * part_t) * inv
                part_s = (jnp.where(wet, sm[c, k, body_rows, :], zero) + lower * part_s) * inv
                tm[c, k, body_rows, :] = part_t
                sm[c, k, body_rows, :] = part_s
                return upper, turn * inv, part_t, part_s

            lax.fori_loop(0, levels, down, (zero, zero, zero, zero))

            def up(i, carry):
                below_t, below_s = carry
                k = levels - 1 - i
                gain = gain_a[k]
                below_t = tm[c, k, body_rows, :] + gain * below_t
                below_s = sm[c, k, body_rows, :] + gain * below_s
                tm[c, k, body_rows, :] = below_t
                sm[c, k, body_rows, :] = below_s
                return below_t, below_s

            lax.fori_loop(0, levels, up, (zero, zero))
            return _

        lax.fori_loop(0, tiles // 2, tracer_tile, 0)

        wait_all(ex1a)
        rim_unpack((k_map, depth_map), rim_w1, rim_e1)
        row_index = lax.axis_index("row")
        south_rim, north_rim = pl.ds(PAD, HALO), pl.ds(top, HALO)
        for inside, rim in ((row_index > 0, south_rim), (row_index < n_rows - 1, north_rim)):
            factor = jnp.where(inside, 1.0, 0.0).astype(F32)
            for c in range(ring):
                k_map[c, rim, :] = k_map[c, rim, :] * factor

        n_blocks = (rows + 2 * HALO) // BLOCK

        def block(i):
            return pl.multiple_of(PAD + BLOCK * i, PAD)

        def thickness(i, _):
            here = pl.ds(block(i), BLOCK)
            for c in range(ring):
                dz_map[c, here, :] = depth_map[c, here, :] / jnp.maximum(k_map[c, here, :], 1.0)
            return _

        lax.fori_loop(0, n_blocks, thickness, 0)

        def faces(i, _):
            here, north = pl.ds(block(i), BLOCK), pl.ds(block(i) + 1, BLOCK)
            k_cell = [k_map[c, here, :] for c in range(ring)]
            dz = [dz_map[c, here, :] for c in range(ring)]
            k_east, dz_east = east(k_cell), east(dz)
            for c in range(ring):
                k_u = jnp.minimum(k_cell[c], k_east[c])
                k_v = jnp.minimum(k_cell[c], k_map[c, north, :])
                dz_u = 0.5 * (dz[c] + dz_east[c])
                dz_v = 0.5 * (dz[c] + dz_map[c, north, :])
                k_out[c, here, :] = k_cell[c]
                ku_map[c, here, :] = k_u
                kv_map[c, here, :] = k_v
                dzu_map[c, here, :] = dz_u
                dzv_map[c, here, :] = dz_v
                wet_map[c, here, :] = jnp.where(k_cell[c] > 0, dt_sub, 0.0)
                hu_map[c, here, :] = dt_sub * (k_u * dz_u)
                hv_map[c, here, :] = dt_sub * (k_v * dz_v)
            return _

        lax.fori_loop(0, n_blocks, faces, 0)

        wait_all(flow_load)

        def mask_tile(c, _):
            for ref, count in ((u, ku_map), (v, kv_map)):
                k_face = count[c, own, :]

                def level(k, done, ref=ref, k_face=k_face):
                    ref[c, k, body_rows, :] = jnp.where(k.astype(F32) < k_face, ref[c, k, body_rows, :], zero)
                    return done

                lax.fori_loop(0, levels, level, 0)
            return _

        lax.fori_loop(0, tiles, mask_tile, 0)

        def edges(firsts, lasts, top_rows, bottom_rows):
            def level(k, carry):
                first, last = carry
                row = pl.ds(k, 1)
                for f, ref in firsts:
                    first = jnp.where(lane == SLOT * f + k, roll(ref[0, k, body_rows, :], SLOT * f + k), first)
                for f, ref in lasts:
                    x = roll(ref[tiles - 1, k, body_rows, :], SLOT * f + k + 1)
                    last = jnp.where(lane == SLOT * f + k, x, last)
                for c in range(tiles):
                    for ref, out in top_rows:
                        out[c, row, :] = ref[c, k, pl.ds(PAD, 1), :]
                    for ref, out in bottom_rows:
                        out[c, row, :] = ref[c, k, pl.ds(PAD + rows - 1, 1), :]
                return first, last

            return lax.fori_loop(0, levels, level, (zero, zero))

        fr_u, fr_v, fr_p = split(first_row)
        lr_u, lr_v = split(last_row)
        flows = ((0, u), (1, v))
        first, last = edges(
            flows + ((2, p),), flows, ((u, fr_u), (v, fr_v), (p, fr_p)), ((u, lr_u), (v, lr_v))
        )
        first_col[...] = first
        last_col[...] = last
        ex2 = remote(
            sem2,
            (first_col, col_e, WEST),
            (last_col, col_w, EAST),
            (first_row, row_n, SOUTH),
            (last_row, row_s, NORTH),
            (last_col.at[pl.ds(0, PAD), :], corner_nw, SOUTH_EAST),
            (first_col.at[pl.ds(rows - PAD, PAD), :], corner_se, NORTH_WEST),
        )
        start_all(ex2)

        wait_all(ex1b)
        rim_unpack((eta_map, tu_map, tv_map), rim_w2, rim_e2)

        def start_fields(i, _):
            here = pl.ds(block(i), BLOCK)
            for ref, count in ((eta_map, k_out), (tu_map, ku_map), (tv_map, kv_map)):
                for c in range(ring):
                    ref[c, here, :] = jnp.where(count[c, here, :] > 0, ref[c, here, :], 0.0)
            return _

        lax.fori_loop(0, n_blocks, start_fields, 0)
        wait_all(ex2)

        def fill(west_east, east_only, west_only, norths, souths):
            def level(k, _):
                here = (halo_tile, k, body_rows, slice(None))
                for ref, f, src_e, src_w in west_east:
                    e = roll(src_e[...], lax.rem(2 * LANES - SLOT * f - k, LANES))
                    w = roll(src_w[...], LANES - 1 - SLOT * f - k)
                    ref[here] = jnp.where(lane < LANES // 2, e, w)
                for ref, f, src in east_only:
                    ref[here] = roll(src[...], LANES - SLOT * f - k)
                for ref, f, src in west_only:
                    ref[here] = roll(src[...], LANES - 1 - SLOT * f - k)
                row = pl.ds(k, 1)
                for c in range(tiles):
                    for ref, src in norths:
                        ref[c, k, pl.ds(PAD + rows, 1), :] = src[c, row, :]
                    for ref, src in souths:
                        ref[c, k, pl.ds(PAD - 1, 1), :] = src[c, row, :]
                return _

            lax.fori_loop(0, levels, level, 0)

        rn_u, rn_v, rn_p = split(row_n)
        rs_u, rs_v = split(row_s)
        fill(
            ((u, 0, col_e, col_w), (v, 1, col_e, col_w)), ((p, 2, col_e),), (),
            ((u, rn_u), (v, rn_v), (p, rn_p)), ((u, rs_u), (v, rs_v)),
        )

        def corners(k, _):
            u[halo_tile, k, pl.ds(PAD + rows, PAD), :] = roll(corner_nw[...], LANES - 1 - k)
            v[halo_tile, k, pl.ds(0, PAD), :] = roll(corner_se[...], LANES - SLOT - k)
            return _

        lax.fori_loop(0, levels, corners, 0)

        quarter = 0.25 * TIME_STEP

        def momentum(k, _):
            for r in range(0, PAD + rows, CROSS_ROWS):
                here, north = pl.ds(r, CROSS_ROWS), pl.ds(r + 1, CROSS_ROWS)
                vv = [v[c, k, here, :] for c in range(ring)]
                v_east = east(vv)
                for c in range(ring):
                    cross[c, here, :] = (vv[c] + v_east[c]) * (u[c, k, here, :] + u[c, k, north, :])
            for r in range(PAD, PAD + rows, FLOW_ROWS):
                here, north, south = pl.ds(r, FLOW_ROWS), pl.ds(r + 1, FLOW_ROWS), pl.ds(r - 1, FLOW_ROWS)
                uu = [u[c, k, here, :] for c in range(ring)]
                square = [x + y for x, y in zip(uu, east(uu))]
                square = [x * x for x in square]
                square_west = west(square)
                xx = [cross[c, here, :] for c in range(ring)]
                x_west = west(xx)
                pp = [p[c, k, here, :] for c in range(ring)]
                p_east = east(pp)
                for c in range(tiles):
                    push = (square[c] - square_west[c]) + (xx[c] - cross[c, south, :])
                    us[c, k, here, :] = uu[c] - (scaled(quarter, push) + (p_east[c] - pp[c]))
                    vv = v[c, k, here, :]
                    b_here = vv + v[c, k, north, :]
                    b_south = vv + v[c, k, south, :]
                    push = (b_here * b_here - b_south * b_south) + (xx[c] - x_west[c])
                    vs[c, k, here, :] = vv - (scaled(quarter, push) + (p[c, k, north, :] - pp[c]))
            return _

        lax.fori_loop(0, levels, momentum, 0)

        nil = jnp.zeros((SOLVE_ROWS, LANES), F32)
        parts = rows // SOLVE_ROWS

        def solve_tile(i, _):
            c, r = i // parts, pl.multiple_of((i % parts) * SOLVE_ROWS, PAD)
            flat, here = pl.ds(core + r, SOLVE_ROWS), pl.ds(PAD + r, SOLVE_ROWS)
            faces = []
            for count, dz in ((ku_map, dzu_map), (kv_map, dzv_map)):
                k_face = count[c, flat, :]
                safe = jnp.where(k_face > 0, dz[c, flat, :], 1.0)
                faces.append((k_face, (TIME_STEP * VISC_KV) / (safe * safe)))

            def down(k, carry):
                kf = k.astype(F32)
                out = []
                for face, ref, gain, state in zip(faces, (us, vs), (gain_a, gain_b), carry):
                    k_face, couple = face
                    lower, keep, part = state
                    upper = jnp.where(kf + 1.0 < k_face, couple, nil)
                    turn = 1.0 + lower * keep
                    inv = 1.0 / (turn + upper)
                    gain[k, pl.ds(0, SOLVE_ROWS), :] = upper * inv
                    part = (jnp.where(kf < k_face, ref[c, k, here, :], nil) + lower * part) * inv
                    ref[c, k, here, :] = part
                    out.append((upper, turn * inv, part))
                return tuple(out)

            lax.fori_loop(0, levels, down, ((nil,) * 3,) * 2)

            def up(j, carry):
                k = levels - 1 - j
                out = []
                for ref, old, gain, state in zip((us, vs), (u, v), (gain_a, gain_b), carry):
                    below, total, change = state
                    below = ref[c, k, here, :] + gain[k, pl.ds(0, SOLVE_ROWS), :] * below
                    ref[c, k, here, :] = below
                    out.append((below, total + below, change + (below - old[c, k, here, :])))
                return tuple(out)

            sums = lax.fori_loop(0, levels, up, ((nil,) * 3,) * 2)
            for dz, total_map, force_map, state in zip((dzu_map, dzv_map), (su_map, sv_map), (fu_map, fv_map), sums):
                _, total, change = state
                total_map[c, flat, :] = dz[c, flat, :] * total
                force_map[c, flat, :] = dz[c, flat, :] * change * (1.0 / TIME_STEP)
            return i

        lax.fori_loop(0, tiles * parts, solve_tile, 0)

        rim_pack((fu_map, fv_map), pk_e3, pk_w3)
        ex3 = rim_copies(force, pk_e3, pk_w3, rim_w3, rim_e3, sem3)
        start_all(ex3)

        lax.fori_loop(tiles // 2, tiles, tracer_tile, 0)

        fr_t4, fr_s4 = split(first_row4)
        lr_v4, lr_t4, lr_s4 = split(last_row4)
        mixed = ((1, tm), (2, sm))
        first, last = edges(
            mixed, ((0, us),) + mixed, ((tm, fr_t4), (sm, fr_s4)), ((vs, lr_v4), (tm, lr_t4), (sm, lr_s4))
        )
        first_col4[...] = first
        last_col4[...] = jnp.where(lane == levels, roll(su_map[tiles - 1, own, :], levels + 1), last)
        for c in range(tiles):
            lr_v4[c, pl.ds(levels, 1), :] = sv_map[c, pl.ds(top - 1, 1), :]
        ex4 = remote(
            sem4,
            (first_col4, col_e4, WEST),
            (last_col4, col_w4, EAST),
            (first_row4, row_n4, SOUTH),
            (last_row4, row_s4, NORTH),
        )
        start_all(ex4)

        wait_all(ex3)
        rim_unpack((fu_map, fv_map), rim_w3, rim_e3)

        def force_fields(i, _):
            here = pl.ds(block(i), BLOCK)
            for ref, count in ((fu_map, ku_map), (fv_map, kv_map)):
                for c in range(ring):
                    ref[c, here, :] = jnp.where(count[c, here, :] > 0, dt_sub * ref[c, here, :], 0.0)
            return _

        lax.fori_loop(0, n_blocks, force_fields, 0)

        def subcycle(low, high):
            def body(n, _):
                tide_u, tide_v = tide[n, 0], tide[n, 1]
                weight = weight_norm * ((n + 1) * (n_sub - n)).astype(F32)
                for r in range(low, high, SUB_ROWS):
                    here, south = pl.ds(r, SUB_ROWS), pl.ds(r - 1, SUB_ROWS)
                    tu = [tu_map[c, here, :] for c in range(ring)]
                    tu_west = west(tu)
                    for c in range(ring):
                        spread = (tu[c] - tu_west[c]) + (tv_map[c, here, :] - tv_map[c, south, :])
                        eta_map[c, here, :] = eta_map[c, here, :] - wet_map[c, here, :] * spread
                for r in range(low, high, SUB_ROWS):
                    here, north = pl.ds(r, SUB_ROWS), pl.ds(r + 1, SUB_ROWS)
                    eta = [eta_map[c, here, :] for c in range(ring)]
                    eta_east = east(eta)
                    averaged = r + SUB_ROWS > core - 1 and r < top
                    for c in range(ring):
                        drive = hu_map[c, here, :] * (tide_u - scaled(GRAVITY, eta_east[c] - eta[c]))
                        tu = tu_map[c, here, :] + (drive + fu_map[c, here, :])
                        tu_map[c, here, :] = tu
                        drive = hv_map[c, here, :] * (tide_v - scaled(GRAVITY, eta_map[c, north, :] - eta[c]))
                        tv = tv_map[c, here, :] + (drive + fv_map[c, here, :])
                        tv_map[c, here, :] = tv
                        if averaged:
                            mu_map[c, here, :] = mu_map[c, here, :] + weight * tu
                            if c < tiles:
                                mv_map[c, here, :] = mv_map[c, here, :] + weight * tv
                return _

            return body

        begin, margin = 0, 0
        while begin < n_sub:
            end = n_sub if margin + PAD >= HALO else min(n_sub, n_sub - (HALO - margin - PAD))
            if end > begin:
                lax.fori_loop(begin, end, subcycle(PAD + margin, flat_rows - PAD - margin), 0)
                begin = end
            margin += PAD

        for ref, out in zip((eta_map, tu_map, tv_map), split(baro_out)):
            for c in range(tiles):
                out[c] = ref[c, own, :]

        wait_all(ex4)
        rn_t4, rn_s4 = split(row_n4)
        rs_v4, rs_t4, rs_s4 = split(row_s4)
        fill(
            ((tm, 1, col_e4, col_w4), (sm, 2, col_e4, col_w4)), (), ((us, 0, col_w4),),
            ((tm, rn_t4), (sm, rn_s4)), ((vs, rs_v4), (tm, rs_t4), (sm, rs_s4)),
        )
        su_map[halo_tile, own, :] = roll(col_w4[...], LANES - 1 - levels)
        for c in range(tiles):
            sv_map[c, pl.ds(core - 1, 1), :] = rs_v4[c, pl.ds(levels, 1), :]
        cu_map, cv_map = split(corr)
        for out, mean_map, total_map, count, dz, n, here in (
            (cu_map, mu_map, su_map, ku_map, dzu_map, ring, own),
            (cv_map, mv_map, sv_map, kv_map, dzv_map, tiles, pl.ds(core - PAD, rows + PAD)),
        ):
            for c in range(n):
                depth = count[c, here, :] * dz[c, here, :]
                safe = jnp.where(depth > 0, depth, 1.0)
                out[c, here, :] = (mean_map[c, here, :] - total_map[c, here, :]) / safe

    group = 4

    def back(us, vs, tm, sm, baro_in, corr, counts, eta_o, tu_o, tv_o, u_o, v_o, t_o, s_o, flux):
        k_map, ku_map, kv_map = split(counts)
        cu_map, cv_map = split(corr)
        fluxes = split(flux)
        for ref, out in zip(split(baro_in), (eta_o, tu_o, tv_o)):
            for c in range(tiles):
                out[:, pl.ds(c * LANES, LANES)] = ref[c]
        half = 0.5 * TIME_STEP

        def level(i, _):
            k = jnp.minimum(pl.program_id(0) * group + i, levels - 1)
            kf = k.astype(F32)
            for r in range(0, PAD + rows, BACK_ROWS):
                here, north = pl.ds(r, BACK_ROWS), pl.ds(r + 1, BACK_ROWS)
                flat = pl.ds(r + core - PAD, BACK_ROWS)
                for c in range(tiles):
                    vv = jnp.where(kf < kv_map[c, flat, :], vs[c, k, here, :] + cv_map[c, flat, :], 0.0)
                    if r >= PAD:
                        v_o[i, pl.ds(r - PAD, BACK_ROWS), pl.ds(c * LANES, LANES)] = vv
                    vv = half * vv
                    for ref, store in zip((tm, sm), fluxes):
                        store[c, here, :] = vv * (ref[c, k, here, :] + ref[c, k, north, :])
            for r in range(PAD, PAD + rows, BACK_ROWS):
                here, south = pl.ds(r, BACK_ROWS), pl.ds(r - 1, BACK_ROWS)
                flat = pl.ds(r - PAD + core, BACK_ROWS)
                out_rows = pl.ds(r - PAD, BACK_ROWS)
                uu = []
                for c in range(ring):
                    x = jnp.where(kf < ku_map[c, flat, :], us[c, k, here, :] + cu_map[c, flat, :], 0.0)
                    if c < tiles:
                        u_o[i, out_rows, pl.ds(c * LANES, LANES)] = x
                    uu.append(half * x)
                for ref, store, out in zip((tm, sm), fluxes, (t_o, s_o)):
                    tt = [ref[c, k, here, :] for c in range(ring)]
                    fx = [x * (y + z) for x, y, z in zip(uu, tt, east(tt))]
                    fx_west = west(fx)
                    for c in range(tiles):
                        spread = (fx[c] - fx_west[c]) + (store[c, here, :] - store[c, south, :])
                        new = jnp.where(kf < k_map[c, flat, :], tt[c] - spread, 0.0)
                        out[i, out_rows, pl.ds(c * LANES, LANES)] = new
            return _

        lax.fori_loop(0, group, level, 0)

    vmem = lambda *shape: pltpu.VMEM(shape, F32)
    flat = lambda n: vmem(n, ring, flat_rows, LANES)
    line = lambda n: vmem(n, tiles, SLOT, LANES)
    cube_buf = vmem(ring, levels, ext_rows, LANES)
    gain_buf = vmem(levels, rows, LANES)
    pack_buf = vmem(3, rows, LANES)
    rim_buf = vmem(3, rows + 2 * HALO, LANES)
    col_buf, corner_buf = vmem(rows, LANES), vmem(PAD, LANES)
    dma = lambda *shape: pltpu.SemaphoreType.DMA(shape)
    shared = [cube_buf, cube_buf, cube_buf, cube_buf, vmem(3, tiles, rows, LANES), flat(2), flat(3)]
    routes = len(COMPASS)
    any_spec = pl.BlockSpec(memory_space=pl.ANY)
    vmem_spec = pl.BlockSpec(memory_space=pltpu.VMEM)
    front_call = pl.pallas_call(
        front,
        name="front",
        out_shape=shared,
        in_specs=[any_spec] * 9 + [pl.BlockSpec(memory_space=pltpu.SMEM)],
        out_specs=[vmem_spec] * len(shared),
        scratch_shapes=[
            cube_buf, cube_buf, cube_buf, gain_buf, gain_buf,
            vmem(ring, ext_rows, LANES), pltpu.VMEM((tiles, rows, LANES), jnp.int32),
            flat(2), flat(3), flat(3), flat(2), flat(3), flat(2), flat(2),
            pack_buf, pack_buf, rim_buf, rim_buf,
            col_buf, col_buf, line(3), line(2),
            col_buf, col_buf, line(3), line(2), corner_buf, corner_buf,
            col_buf, col_buf, line(2), line(3),
            col_buf, col_buf, line(2), line(3),
            dma(4, tiles), dma(5, tiles), dma(2, routes), dma(2, routes), dma(2, routes), dma(2, routes), dma(2, routes),
        ],
        compiler_params=pltpu.CompilerParams(
            collective_id=0, has_side_effects=True, vmem_limit_bytes=31 * MIB
        ),
    )
    plane_out = pl.BlockSpec((rows, cols), lambda i: (0, 0))
    cube_out = pl.BlockSpec((group, rows, cols), lambda i: (i, 0, 0))
    plane_shape = jax.ShapeDtypeStruct((rows, cols), F32)
    cube_shape = jax.ShapeDtypeStruct((levels, rows, cols), F32)
    back_call = pl.pallas_call(
        back,
        name="back",
        grid=(pl.cdiv(levels, group),),
        out_shape=[plane_shape] * 3 + [cube_shape] * 4,
        in_specs=[vmem_spec] * len(shared),
        out_specs=[plane_out] * 3 + [cube_out] * 4,
        scratch_shapes=[vmem(2, tiles, ext_rows, LANES)],
        compiler_params=pltpu.CompilerParams(vmem_limit_bytes=8 * MIB),
    )
    return front_call, back_call


def solution(mesh):
    def local_step(vel_u, vel_v, temperature, salinity, sea_level, trans_u, trans_v, bathymetry, kmt_levels, tide_force):
        levels, rows, cols = vel_u.shape
        front_call, back_call = kernels(mesh, levels, rows, cols, tide_force.shape[0])
        shared = front_call(
            vel_u, vel_v, temperature, salinity, sea_level, trans_u, trans_v, bathymetry, kmt_levels, tide_force
        )
        return tuple(back_call(*shared))

    spec_cube = P(None, "row", "col")
    spec_plane = P("row", "col")
    return jax.shard_map(
        local_step,
        mesh=mesh,
        in_specs=(spec_cube,) * 4 + (spec_plane,) * 5 + (P(None, None),),
        out_specs=(spec_plane,) * 3 + (spec_cube,) * 4,
        check_vma=False,
    )
```

time: 1460 us -> 98.5 us (0.07); the launches traced: 1440 us -> 98.2 us
  other arithmetic: 671 us -> 0 us
  starting transfers between devices: 352 us -> 0 us
  waiting for transfers between devices: 331 us -> 0 us
  Pallas kernels: 0 us -> 96.2 us
  local copies, waits for them, and re-layouts: 82.9 us -> 1.37 us
    dynamic_update_slice x248 -> x0, other arithmetic: 451 us -> none  [column_solve(): _, (gains, parts) = lax.scan(forward, start, (lower, diag, upper, source))]
    ppermute x195 -> x0, starting transfers between devices: 352 us -> none  [the longest x34 170 us: halo_swap(): from_south = lax.ppermute(wide[..., -1:, :], 'row', south_perm)]
    ppermute x195 -> x0, waiting for transfers between devices: 331 us -> none  [the longest x64 126 us: halo_swap(): from_east = lax.ppermute(field[..., :1], 'col', east_perm)]
    mul x44 -> x0, other arithmetic: 130 us -> none  [the longest x1 24.2 us: baroclinic_predict(): mask_u * (vel_um + TIME_STEP * tend_u)]
    pallas_call x0 -> x2, Pallas kernels: none -> 96.2 us  [the longest x1 79.2 us: local_step(): front_call(vel_u, vel_v, temperature, salinity, sea_level, trans_u, trans...]
    another operation x13 -> x0, local copies, waits for them, and re-layouts: 32.3 us -> none
    concatenate x65 -> x0, other arithmetic: 26.1 us -> none  [the longest x3 19.6 us: column_solve(): lower = jnp.concatenate([edge, couple], axis=0)]
    slice x67 -> x0, local copies, waits for them, and re-layouts: 25.6 us -> none  [the longest x65 21.5 us: halo_swap(): from_west = lax.ppermute(field[..., -1:], 'col', west_perm)]
  transfers between devices with their start and end apart: 195 -> 0, of which waited for: 183 -> 0; matrix products, arithmetic and copies ran while one was open for 4% -> 0% of each run, Pallas kernels for 0% -> 0%
where the time goes in v1:
time: 98.5 us; the launch traced here: 98.2 us
  Pallas kernels  96.2 us (98%)
  local copies, waits for them, and re-layouts  1.37 us (1%)
    pallas_call x1, Pallas kernels, local_step(): front_call(vel_u, vel_v, temperature, salinity, sea_level, trans_u, trans...  79.2 us
    pallas_call x1, Pallas kernels, local_step(): return tuple(back_call(*shared))  17 us

profile of v1, /device:TPU:0, one launch (start us, length us, event | category | flops | bytes accessed | tf_op | source)
XLA Modules:
  0.0 98.2 jit_solution(6784043719506092583)
XLA Ops:
  0.6 1.4 %copy.17.tide = f32[30,2]{1,0:T(8,128)} copy(f32[30,2]{0,1:T(2,128)} %param.19) | data formatting | bytes 480 | tf_op args[9]
  2.0 79.2 %front.1 = (f32[5,31,80,128]{3,2,1,0:T(8,128)S(1)}, f32[5,31,80,128]{3,2,1,0:T(8,128)S(1)}, f32[5,31,80,128]{3,2,1,0:T(8,128)S(1)}, f32[5,31,80,128]{3,2,1,0:T(8...) custom-call(f32[31,64,512]{2,1,0:T(8,128)} %u_hbm.1, ...), custom_call_target="tpu_custom_call" | custom-call | tf_op jit(solution)/shard_map/front/pallas_call | solution.py:693
  81.2 17.0 %back.1 = (f32[64,512]{1,0:T(8,128)}, f32[64,512]{1,0:T(8,128)}, f32[64,512]{1,0:T(8,128)}, f32[31,64,512]{2,1,0:T(8,128)}, f32[31,64,512]{2,1,0:T(8,128)}, /*in...) custom-call(f32[5,31,80,128]{3,2,1,0:T(8,128)S(1)} %get-tuple-element.14.us, f32[5,31,80,128]{3,2,1,0:T(8,128)S(1)} %get-tuple-element.15.vs, ...), custom_call_target="tpu_custom_call" | custom-call | tf_op jit(solution)/shard_map/back/pallas_call | solution.py:696

commit v2 on v1

--- a/solution.py
+++ b/solution.py
@@ -17,17 +17,18 @@
 LANES = 128
 HALO = 32
 PAD = 8
+NEAR = 16
 F32 = jnp.float32
 NORTH, SOUTH, EAST, WEST = (1, 0), (-1, 0), (0, 1), (0, -1)
 NORTH_EAST, NORTH_WEST, SOUTH_EAST, SOUTH_WEST = (1, 1), (1, -1), (-1, 1), (-1, -1)
 COMPASS = (NORTH, SOUTH, EAST, WEST, NORTH_EAST, NORTH_WEST, SOUTH_EAST, SOUTH_WEST)
 SLOT = 32
 BLOCK = 16
-CROSS_ROWS = 8
-FLOW_ROWS = 8
+CROSS_ROWS = 72
+FLOW_ROWS = 64
 SOLVE_ROWS = 32
 SUB_ROWS = 16
-BACK_ROWS = 8
+BACK_ROWS = 16
 MIB = 2**20
 
 
@@ -107,40 +108,45 @@
         pack_east[...] = last
         pack_west[...] = first
 
-    def rim_copies(main, pack_east, pack_west, from_west, from_east, sems):
-        inner = pl.ds(0, tiles)
-        low, high = pl.ds(core, HALO), pl.ds(top - HALO, HALO)
-        p_low, p_all, p_high = pl.ds(0, HALO), pl.ds(0, rows), pl.ds(rows - HALO, HALO)
-        d_low, d_all, d_high = pl.ds(0, HALO), pl.ds(HALO, rows), pl.ds(HALO + rows, HALO)
-        every = pl.ds(0, main.shape[0])
+    def row_rims(main, sems, reach, skip=0):
+        every, inner, n = pl.ds(0, main.shape[0]), pl.ds(0, tiles), reach - skip
         return remote(
             sems,
-            (main.at[every, inner, high, :], main.at[every, inner, pl.ds(PAD, HALO), :], NORTH),
-            (main.at[every, inner, low, :], main.at[every, inner, pl.ds(top, HALO), :], SOUTH),
-            (pack_east.at[p_all, :], from_west.at[d_all, :], EAST),
-            (pack_west.at[p_all, :], from_east.at[d_all, :], WEST),
+            (main.at[every, inner, pl.ds(top - reach, n), :], main.at[every, inner, pl.ds(core - reach, n), :], NORTH),
+            (main.at[every, inner, pl.ds(core + skip, n), :], main.at[every, inner, pl.ds(top + skip, n), :], SOUTH),
+        )
+
+    def column_rims(pack_east, pack_west, from_west, from_east, sems):
+        own_rows = pl.ds(HALO, rows)
+        return remote(sems, (pack_east, from_west.at[own_rows, :], EAST), (pack_west, from_east.at[own_rows, :], WEST))
+
+    def corner_rims(pack_east, pack_west, from_west, from_east, sems, reach, skip=0):
+        n = reach - skip
+        p_high, p_low = pl.ds(rows - reach, n), pl.ds(skip, n)
+        d_low, d_high = pl.ds(HALO - reach, n), pl.ds(HALO + rows + skip, n)
+        return remote(
+            sems,
             (pack_east.at[p_high, :], from_west.at[d_low, :], NORTH_EAST),
             (pack_west.at[p_high, :], from_east.at[d_low, :], NORTH_WEST),
             (pack_east.at[p_low, :], from_west.at[d_high, :], SOUTH_EAST),
             (pack_west.at[p_low, :], from_east.at[d_high, :], SOUTH_WEST),
         )
 
-    def rim_unpack(maps, from_west, from_east):
-        n = rows + 2 * HALO
+    def rim_unpack(maps, from_west, from_east, start, n):
         easterly = lane_iota(n) < LANES // 2
+        here = pl.ds(start - PAD, n)
         for f, ref in enumerate(maps):
-            e = roll(from_east[...], (LANES - HALO * f) % LANES)
-            w = roll(from_west[...], LANES - HALO - HALO * f)
-            ref[halo_tile, pl.ds(PAD, n), :] = jnp.where(easterly, e, w)
+            e = roll(from_east[here, :], (LANES - HALO * f) % LANES)
+            w = roll(from_west[here, :], LANES - HALO - HALO * f)
+            ref[halo_tile, pl.ds(start, n), :] = jnp.where(easterly, e, w)
 
     def front(
-        u_hbm, v_hbm, t_hbm, s_hbm, eta_hbm, tu_hbm, tv_hbm, depth_hbm, kmt_hbm, tide,
+        u_hbm, v_hbm, t_hbm, s_hbm, eta_hbm, tu_hbm, tv_hbm, depth_hbm, kmt_hbm, tide_hbm,
         us, vs, tm, sm, baro_out, corr, counts,
         u, v, p, gain_a, gain_b, cross, kmt_int, geo, thick, baro, force, coef, mean, depth_sum,
-        pk_e, pk_w, rim_w, rim_e, first_col, last_col, first_row, last_row,
-        col_e, col_w, row_n, row_s, corner_nw, corner_se,
-        col_e4, col_w4, row_n4, row_s4, first_col4, last_col4, first_row4, last_row4,
-        load_sems, plane_sems, sem1a, sem1b, sem2, sem3, sem4,
+        pk_e, pk_w, rim_w, rim_e, cols, cols_e, cols_w, cols_in, first_row, last_row,
+        row_n, row_s, corner_nw, corner_se, first_row4, last_row4, row_n4, row_s4, tide,
+        load_sems, plane_sems, tide_sem, sem_near, sem_far, sem_baro, sem_uvp, sem_ts, sem_force, sem_star,
     ):
         k_map, depth_map = split(geo)
         eta_map, tu_map, tv_map = split(baro)
@@ -186,7 +192,12 @@
         )
         tracer_load = cube_load(sem_t, t_hbm, tm) + cube_load(sem_s, s_hbm, sm)
         flow_load = cube_load(sem_u, u_hbm, u) + cube_load(sem_v, v_hbm, v)
-        start_all(geo_load + baro_load + tracer_load + flow_load)
+        tide_load = pltpu.make_async_copy(tide_hbm, tide, tide_sem)
+        start_all(geo_load)
+        start_all(tracer_load)
+        start_all(flow_load)
+        start_all(baro_load)
+        tide_load.start()
 
         zero_rows = jnp.zeros((PAD, LANES), F32)
         for ref in (k_map, depth_map, dz_map, eta_map, tu_map, tv_map):
@@ -202,14 +213,12 @@
             k_map[c, own, :] = kmt_int[c].astype(F32)
         rim_pack((k_map, depth_map), pk_e1, pk_w1)
         pl.semaphore_wait(barrier, len(COMPASS))
-        ex1a = rim_copies(geo, pk_e1, pk_w1, rim_w1, rim_e1, sem1a)
-        start_all(ex1a)
-        wait_all(baro_load)
-        rim_pack((eta_map, tu_map, tv_map), pk_e2, pk_w2)
-        ex1b = rim_copies(baro, pk_e2, pk_w2, rim_w2, rim_e2, sem1b)
-        start_all(ex1b)
-
-        wait_all(tracer_load)
+        near_rows, near_cols, near_corners = split(sem_near)
+        near = row_rims(geo, near_rows, NEAR)
+        near += column_rims(pk_e1, pk_w1, rim_w1, rim_e1, near_cols)
+        near += corner_rims(pk_e1, pk_w1, rim_w1, rim_e1, near_corners, NEAR)
+        start_all(near)
+
         rho_s, rho_t = 0.5 * BETA_S, 0.5 * ALPHA_T
         rho_0 = rho_t * T_REF - rho_s * S_REF
 
@@ -227,7 +236,60 @@
             lax.fori_loop(0, levels, level, zero)
             return _
 
-        lax.fori_loop(0, tiles, pressure_tile, 0)
+        for c in range(tiles):
+            wait_all([tracer_load[c], tracer_load[tiles + c]])
+            pressure_tile(c, 0)
+
+        def edges(columns, top_rows, bottom_rows):
+            def level(k, packed):
+                row = pl.ds(k, 1)
+                out = []
+                for pair, acc in zip(columns, packed):
+                    for f, ref in pair:
+                        slot = SLOT * f + k
+                        both = jnp.where(lane < LANES // 2, ref[0, k, body_rows, :], ref[tiles - 1, k, body_rows, :])
+                        acc = jnp.where(lane // 2 == slot, roll(both, 2 * slot + 1), acc)
+                    out.append(acc)
+                for c in range(tiles):
+                    for ref, dst in top_rows:
+                        dst[c, row, :] = ref[c, k, pl.ds(PAD, 1), :]
+                    for ref, dst in bottom_rows:
+                        dst[c, row, :] = ref[c, k, pl.ds(PAD + rows - 1, 1), :]
+                return tuple(out)
+
+            return lax.fori_loop(0, levels, level, (zero,) * len(columns))
+
+        wait_all(flow_load)
+        cols_uv, cols_p, cols_ts, cols_us = split(cols)
+        east_uv, east_p, east_ts = split(cols_e)
+        west_uv, west_ts, west_us = split(cols_w)
+        fr_u, fr_v, fr_p = split(first_row)
+        lr_u, lr_v = split(last_row)
+        cols_uv[...], cols_p[...] = edges(
+            (((0, u), (1, v)), ((0, p),)), ((u, fr_u), (v, fr_v), (p, fr_p)), ((u, lr_u), (v, lr_v))
+        )
+        ex_uvp = remote(
+            sem_uvp,
+            (cols_uv, east_uv, WEST),
+            (cols_p, east_p, WEST),
+            (cols_uv, west_uv, EAST),
+            (first_row, row_n, SOUTH),
+            (last_row, row_s, NORTH),
+            (cols_uv.at[pl.ds(0, PAD), :], corner_nw, SOUTH_EAST),
+            (cols_uv.at[pl.ds(rows - PAD, PAD), :], corner_se, NORTH_WEST),
+        )
+        start_all(ex_uvp)
+
+        wait_all(baro_load)
+        rim_pack((eta_map, tu_map, tv_map), pk_e2, pk_w2)
+        far_rows, far_corners = split(sem_far)
+        baro_rows, baro_cols, baro_corners = split(sem_baro)
+        far = row_rims(geo, far_rows, HALO, NEAR)
+        far += corner_rims(pk_e1, pk_w1, rim_w1, rim_e1, far_corners, HALO, NEAR)
+        far += row_rims(baro, baro_rows, HALO)
+        far += column_rims(pk_e2, pk_w2, rim_w2, rim_e2, baro_cols)
+        far += corner_rims(pk_e2, pk_w2, rim_w2, rim_e2, baro_corners, HALO)
+        start_all(far)
 
         def tracer_tile(c, _):
             k_cell = k_map[c, own, :]
@@ -264,32 +326,38 @@
             lax.fori_loop(0, levels, up, (zero, zero))
             return _
 
-        lax.fori_loop(0, tiles // 2, tracer_tile, 0)
-
-        wait_all(ex1a)
-        rim_unpack((k_map, depth_map), rim_w1, rim_e1)
+        lax.fori_loop(0, tiles, tracer_tile, 0)
+        fr_t4, fr_s4 = split(first_row4)
+        lr_t4, lr_s4, lr_v4 = split(last_row4)
+        rn_t4, rn_s4 = split(row_n4)
+        rs_t4, rs_s4, rs_v4 = split(row_s4)
+        (packed,) = edges((((0, tm), (1, sm)),), ((tm, fr_t4), (sm, fr_s4)), ((tm, lr_t4), (sm, lr_s4)))
+        cols_ts[...] = packed
+        two = pl.ds(0, 2)
+        ex_ts = remote(
+            sem_ts,
+            (cols_ts, east_ts, WEST),
+            (cols_ts, west_ts, EAST),
+            (first_row4, row_n4, SOUTH),
+            (last_row4.at[two], row_s4.at[two], NORTH),
+        )
+        start_all(ex_ts)
+
         row_index = lax.axis_index("row")
-        south_rim, north_rim = pl.ds(PAD, HALO), pl.ds(top, HALO)
-        for inside, rim in ((row_index > 0, south_rim), (row_index < n_rows - 1, north_rim)):
-            factor = jnp.where(inside, 1.0, 0.0).astype(F32)
-            for c in range(ring):
-                k_map[c, rim, :] = k_map[c, rim, :] * factor
-
-        n_blocks = (rows + 2 * HALO) // BLOCK
-
-        def block(i):
-            return pl.multiple_of(PAD + BLOCK * i, PAD)
-
-        def thickness(i, _):
-            here = pl.ds(block(i), BLOCK)
+
+        def wall(low, n, inside):
+            @pl.when(jnp.logical_not(inside))
+            def _():
+                for c in range(ring):
+                    k_map[c, pl.ds(low, n), :] = jnp.zeros((n, LANES), F32)
+
+        def thickness(start, n):
+            here = pl.ds(start, n)
             for c in range(ring):
                 dz_map[c, here, :] = depth_map[c, here, :] / jnp.maximum(k_map[c, here, :], 1.0)
-            return _
-
-        lax.fori_loop(0, n_blocks, thickness, 0)
-
-        def faces(i, _):
-            here, north = pl.ds(block(i), BLOCK), pl.ds(block(i) + 1, BLOCK)
+
+        def faces(start, n):
+            here, north = pl.ds(start, n), pl.ds(start + 1, n)
             k_cell = [k_map[c, here, :] for c in range(ring)]
             dz = [dz_map[c, here, :] for c in range(ring)]
             k_east, dz_east = east(k_cell), east(dz)
@@ -306,11 +374,17 @@
                 wet_map[c, here, :] = jnp.where(k_cell[c] > 0, dt_sub, 0.0)
                 hu_map[c, here, :] = dt_sub * (k_u * dz_u)
                 hv_map[c, here, :] = dt_sub * (k_v * dz_v)
-            return _
-
-        lax.fori_loop(0, n_blocks, faces, 0)
-
-        wait_all(flow_load)
+
+        def in_blocks(work, start, n, size=BLOCK):
+            lax.fori_loop(0, n // size, lambda i, _: (work(pl.multiple_of(start + size * i, PAD), size), _)[1], 0)
+
+        far_low, far_high, far_n = PAD, top + NEAR, HALO - NEAR
+        wait_all(near)
+        rim_unpack((k_map, depth_map), rim_w1, rim_e1, core - NEAR, rows + 2 * NEAR)
+        wall(core - NEAR, NEAR, row_index > 0)
+        wall(top, NEAR, row_index < n_rows - 1)
+        in_blocks(thickness, core - NEAR, rows + 2 * NEAR)
+        in_blocks(faces, core - PAD, rows + 2 * PAD)
 
         def mask_tile(c, _):
             for ref, count in ((u, ku_map), (v, kv_map)):
@@ -325,87 +399,44 @@
 
         lax.fori_loop(0, tiles, mask_tile, 0)
 
-        def edges(firsts, lasts, top_rows, bottom_rows):
-            def level(k, carry):
-                first, last = carry
-                row = pl.ds(k, 1)
-                for f, ref in firsts:
-                    first = jnp.where(lane == SLOT * f + k, roll(ref[0, k, body_rows, :], SLOT * f + k), first)
-                for f, ref in lasts:
-                    x = roll(ref[tiles - 1, k, body_rows, :], SLOT * f + k + 1)
-                    last = jnp.where(lane == SLOT * f + k, x, last)
-                for c in range(tiles):
-                    for ref, out in top_rows:
-                        out[c, row, :] = ref[c, k, pl.ds(PAD, 1), :]
-                    for ref, out in bottom_rows:
-                        out[c, row, :] = ref[c, k, pl.ds(PAD + rows - 1, 1), :]
-                return first, last
-
-            return lax.fori_loop(0, levels, level, (zero, zero))
-
-        fr_u, fr_v, fr_p = split(first_row)
-        lr_u, lr_v = split(last_row)
-        flows = ((0, u), (1, v))
-        first, last = edges(
-            flows + ((2, p),), flows, ((u, fr_u), (v, fr_v), (p, fr_p)), ((u, lr_u), (v, lr_v))
-        )
-        first_col[...] = first
-        last_col[...] = last
-        ex2 = remote(
-            sem2,
-            (first_col, col_e, WEST),
-            (last_col, col_w, EAST),
-            (first_row, row_n, SOUTH),
-            (last_row, row_s, NORTH),
-            (last_col.at[pl.ds(0, PAD), :], corner_nw, SOUTH_EAST),
-            (first_col.at[pl.ds(rows - PAD, PAD), :], corner_se, NORTH_WEST),
-        )
-        start_all(ex2)
-
-        wait_all(ex1b)
-        rim_unpack((eta_map, tu_map, tv_map), rim_w2, rim_e2)
-
-        def start_fields(i, _):
-            here = pl.ds(block(i), BLOCK)
-            for ref, count in ((eta_map, k_out), (tu_map, ku_map), (tv_map, kv_map)):
-                for c in range(ring):
-                    ref[c, here, :] = jnp.where(count[c, here, :] > 0, ref[c, here, :], 0.0)
-            return _
-
-        lax.fori_loop(0, n_blocks, start_fields, 0)
-        wait_all(ex2)
-
-        def fill(west_east, east_only, west_only, norths, souths):
+        def fill(columns, norths, souths):
+            def masked(x, k, count, tile, here):
+                return x if count is None else jnp.where(k.astype(F32) < count[tile, here, :], x, 0.0)
+
             def level(k, _):
-                here = (halo_tile, k, body_rows, slice(None))
-                for ref, f, src_e, src_w in west_east:
-                    e = roll(src_e[...], lax.rem(2 * LANES - SLOT * f - k, LANES))
-                    w = roll(src_w[...], LANES - 1 - SLOT * f - k)
-                    ref[here] = jnp.where(lane < LANES // 2, e, w)
-                for ref, f, src in east_only:
-                    ref[here] = roll(src[...], LANES - SLOT * f - k)
-                for ref, f, src in west_only:
-                    ref[here] = roll(src[...], LANES - 1 - SLOT * f - k)
+                for ref, f, src, count in columns:
+                    x = roll(src[...], LANES - 1 - 2 * (SLOT * f + k))
+                    ref[halo_tile, k, body_rows, :] = masked(x, k, count, halo_tile, own)
                 row = pl.ds(k, 1)
                 for c in range(tiles):
-                    for ref, src in norths:
-                        ref[c, k, pl.ds(PAD + rows, 1), :] = src[c, row, :]
-                    for ref, src in souths:
-                        ref[c, k, pl.ds(PAD - 1, 1), :] = src[c, row, :]
+                    for ref, src, count in norths:
+                        x = masked(src[c, row, :], k, count, c, pl.ds(top, 1))
+                        ref[c, k, pl.ds(PAD + rows, 1), :] = x
+                    for ref, src, count in souths:
+                        x = masked(src[c, row, :], k, count, c, pl.ds(core - 1, 1))
+                        ref[c, k, pl.ds(PAD - 1, 1), :] = x
                 return _
 
             lax.fori_loop(0, levels, level, 0)
 
+        odd = lane % 2 == 1
+        in_uv, in_ts = split(cols_in)
+        wait_all(ex_uvp)
+        in_uv[...] = jnp.where(odd, east_uv[...], west_uv[...])
         rn_u, rn_v, rn_p = split(row_n)
         rs_u, rs_v = split(row_s)
         fill(
-            ((u, 0, col_e, col_w), (v, 1, col_e, col_w)), ((p, 2, col_e),), (),
-            ((u, rn_u), (v, rn_v), (p, rn_p)), ((u, rs_u), (v, rs_v)),
+            ((u, 0, in_uv, ku_map), (v, 1, in_uv, kv_map), (p, 0, east_p, None)),
+            ((u, rn_u, ku_map), (v, rn_v, kv_map), (p, rn_p, None)),
+            ((u, rs_u, ku_map), (v, rs_v, kv_map)),
         )
 
         def corners(k, _):
-            u[halo_tile, k, pl.ds(PAD + rows, PAD), :] = roll(corner_nw[...], LANES - 1 - k)
-            v[halo_tile, k, pl.ds(0, PAD), :] = roll(corner_se[...], LANES - SLOT - k)
+            kf = k.astype(F32)
+            x = roll(corner_nw[...], LANES - 1 - 2 * k)
+            u[halo_tile, k, pl.ds(PAD + rows, PAD), :] = jnp.where(kf < ku_map[halo_tile, pl.ds(top, PAD), :], x, 0.0)
+            x = roll(corner_se[...], LANES - 1 - 2 * (SLOT + k))
+            v[halo_tile, k, pl.ds(0, PAD), :] = jnp.where(kf < kv_map[halo_tile, pl.ds(core - PAD, PAD), :], x, 0.0)
             return _
 
         lax.fori_loop(0, levels, corners, 0)
@@ -444,8 +475,8 @@
         nil = jnp.zeros((SOLVE_ROWS, LANES), F32)
         parts = rows // SOLVE_ROWS
 
-        def solve_tile(i, _):
-            c, r = i // parts, pl.multiple_of((i % parts) * SOLVE_ROWS, PAD)
+        def solve_part(c, i):
+            r = pl.multiple_of(i * SOLVE_ROWS, PAD)
             flat, here = pl.ds(core + r, SOLVE_ROWS), pl.ds(PAD + r, SOLVE_ROWS)
             faces = []
             for count, dz in ((ku_map, dzu_map), (kv_map, dzv_map)):
@@ -485,46 +516,70 @@
                 _, total, change = state
                 total_map[c, flat, :] = dz[c, flat, :] * total
                 force_map[c, flat, :] = dz[c, flat, :] * change * (1.0 / TIME_STEP)
-            return i
-
-        lax.fori_loop(0, tiles * parts, solve_tile, 0)
-
-        rim_pack((fu_map, fv_map), pk_e3, pk_w3)
-        ex3 = rim_copies(force, pk_e3, pk_w3, rim_w3, rim_e3, sem3)
-        start_all(ex3)
-
-        lax.fori_loop(tiles // 2, tiles, tracer_tile, 0)
-
-        fr_t4, fr_s4 = split(first_row4)
-        lr_v4, lr_t4, lr_s4 = split(last_row4)
-        mixed = ((1, tm), (2, sm))
-        first, last = edges(
-            mixed, ((0, us),) + mixed, ((tm, fr_t4), (sm, fr_s4)), ((vs, lr_v4), (tm, lr_t4), (sm, lr_s4))
-        )
-        first_col4[...] = first
-        last_col4[...] = jnp.where(lane == levels, roll(su_map[tiles - 1, own, :], levels + 1), last)
+
+        force_rows, force_cols, force_corners = split(sem_force)
+        ex3 = []
+        for step, c in enumerate((0, tiles - 1) + tuple(range(1, tiles - 1))):
+            lax.fori_loop(0, parts, lambda i, _: (solve_part(c, i), _)[1], 0)
+            low, high, every = pl.ds(core, HALO), pl.ds(top - HALO, HALO), pl.ds(0, 2)
+            sent = remote(
+                force_rows.at[pl.ds(0, 2), pl.ds(2 * step, 2)],
+                (force.at[every, c, high, :], force.at[every, c, pl.ds(PAD, HALO), :], NORTH),
+                (force.at[every, c, low, :], force.at[every, c, pl.ds(top, HALO), :], SOUTH),
+            )
+            if step == 1:
+                rim_pack((fu_map, fv_map), pk_e3, pk_w3)
+                sent += column_rims(pk_e3, pk_w3, rim_w3, rim_e3, force_cols)
+                sent += corner_rims(pk_e3, pk_w3, rim_w3, rim_e3, force_corners, HALO)
+            start_all(sent)
+            ex3 += sent
+
+        (packed,) = edges((((0, us),),), (), ((vs, lr_v4),))
+        cols_us[...] = jnp.where(lane // 2 == levels, roll(su_map[tiles - 1, own, :], 2 * levels + 1), packed)
         for c in range(tiles):
             lr_v4[c, pl.ds(levels, 1), :] = sv_map[c, pl.ds(top - 1, 1), :]
-        ex4 = remote(
-            sem4,
-            (first_col4, col_e4, WEST),
-            (last_col4, col_w4, EAST),
-            (first_row4, row_n4, SOUTH),
-            (last_row4, row_s4, NORTH),
-        )
-        start_all(ex4)
+        ex_star = remote(sem_star, (cols_us, west_us, EAST), (lr_v4, rs_v4, NORTH))
+        start_all(ex_star)
+
+        wait_all(ex_ts)
+        in_ts[...] = jnp.where(odd, east_ts[...], west_ts[...])
+        fill(
+            ((tm, 0, in_ts, None), (sm, 1, in_ts, None)),
+            ((tm, rn_t4, None), (sm, rn_s4, None)),
+            ((tm, rs_t4, None), (sm, rs_s4, None)),
+        )
+
+        wait_all(far)
+        for start in (far_low, far_high):
+            rim_unpack((k_map, depth_map), rim_w1, rim_e1, start, far_n)
+        wall(far_low, far_n, row_index > 0)
+        wall(far_high, far_n, row_index < n_rows - 1)
+        in_blocks(thickness, far_low, far_n, PAD)
+        in_blocks(thickness, far_high, far_n, PAD)
+        in_blocks(faces, PAD, HALO - PAD, PAD)
+        in_blocks(faces, top + PAD, HALO - PAD, PAD)
+        full_n = rows + 2 * HALO
+        rim_unpack((eta_map, tu_map, tv_map), rim_w2, rim_e2, PAD, full_n)
+
+        def start_fields(start, n):
+            here = pl.ds(start, n)
+            for ref, count in ((eta_map, k_out), (tu_map, ku_map), (tv_map, kv_map)):
+                for c in range(ring):
+                    ref[c, here, :] = jnp.where(count[c, here, :] > 0, ref[c, here, :], 0.0)
+
+        in_blocks(start_fields, PAD, full_n)
+        tide_load.wait()
 
         wait_all(ex3)
-        rim_unpack((fu_map, fv_map), rim_w3, rim_e3)
-
-        def force_fields(i, _):
-            here = pl.ds(block(i), BLOCK)
+        rim_unpack((fu_map, fv_map), rim_w3, rim_e3, PAD, full_n)
+
+        def force_fields(start, n):
+            here = pl.ds(start, n)
             for ref, count in ((fu_map, ku_map), (fv_map, kv_map)):
                 for c in range(ring):
                     ref[c, here, :] = jnp.where(count[c, here, :] > 0, dt_sub * ref[c, here, :], 0.0)
-            return _
-
-        lax.fori_loop(0, n_blocks, force_fields, 0)
+
+        in_blocks(force_fields, PAD, full_n)
 
         def subcycle(low, high):
             def body(n, _):
@@ -569,14 +624,9 @@
             for c in range(tiles):
                 out[c] = ref[c, own, :]
 
-        wait_all(ex4)
-        rn_t4, rn_s4 = split(row_n4)
-        rs_v4, rs_t4, rs_s4 = split(row_s4)
-        fill(
-            ((tm, 1, col_e4, col_w4), (sm, 2, col_e4, col_w4)), (), ((us, 0, col_w4),),
-            ((tm, rn_t4), (sm, rn_s4)), ((vs, rs_v4), (tm, rs_t4), (sm, rs_s4)),
-        )
-        su_map[halo_tile, own, :] = roll(col_w4[...], LANES - 1 - levels)
+        wait_all(ex_star)
+        fill(((us, 0, west_us, None),), (), ((vs, rs_v4, None),))
+        su_map[halo_tile, own, :] = roll(west_us[...], LANES - 1 - 2 * levels)
         for c in range(tiles):
             sv_map[c, pl.ds(core - 1, 1), :] = rs_v4[c, pl.ds(levels, 1), :]
         cu_map, cv_map = split(corr)
@@ -603,13 +653,13 @@
         def level(i, _):
             k = jnp.minimum(pl.program_id(0) * group + i, levels - 1)
             kf = k.astype(F32)
-            for r in range(0, PAD + rows, BACK_ROWS):
-                here, north = pl.ds(r, BACK_ROWS), pl.ds(r + 1, BACK_ROWS)
-                flat = pl.ds(r + core - PAD, BACK_ROWS)
+            for r in range(0, PAD + rows, PAD):
+                here, north = pl.ds(r, PAD), pl.ds(r + 1, PAD)
+                flat = pl.ds(r + core - PAD, PAD)
                 for c in range(tiles):
                     vv = jnp.where(kf < kv_map[c, flat, :], vs[c, k, here, :] + cv_map[c, flat, :], 0.0)
                     if r >= PAD:
-                        v_o[i, pl.ds(r - PAD, BACK_ROWS), pl.ds(c * LANES, LANES)] = vv
+                        v_o[i, pl.ds(r - PAD, PAD), pl.ds(c * LANES, LANES)] = vv
                     vv = half * vv
                     for ref, store in zip((tm, sm), fluxes):
                         store[c, here, :] = vv * (ref[c, k, here, :] + ref[c, k, north, :])
@@ -645,25 +695,25 @@
     col_buf, corner_buf = vmem(rows, LANES), vmem(PAD, LANES)
     dma = lambda *shape: pltpu.SemaphoreType.DMA(shape)
     shared = [cube_buf, cube_buf, cube_buf, cube_buf, vmem(3, tiles, rows, LANES), flat(2), flat(3)]
-    routes = len(COMPASS)
+    routes = 7
     any_spec = pl.BlockSpec(memory_space=pl.ANY)
     vmem_spec = pl.BlockSpec(memory_space=pltpu.VMEM)
     front_call = pl.pallas_call(
         front,
         name="front",
         out_shape=shared,
-        in_specs=[any_spec] * 9 + [pl.BlockSpec(memory_space=pltpu.SMEM)],
+        in_specs=[any_spec] * 10,
         out_specs=[vmem_spec] * len(shared),
         scratch_shapes=[
             cube_buf, cube_buf, cube_buf, gain_buf, gain_buf,
             vmem(ring, ext_rows, LANES), pltpu.VMEM((tiles, rows, LANES), jnp.int32),
             flat(2), flat(3), flat(3), flat(2), flat(3), flat(2), flat(2),
             pack_buf, pack_buf, rim_buf, rim_buf,
-            col_buf, col_buf, line(3), line(2),
-            col_buf, col_buf, line(3), line(2), corner_buf, corner_buf,
-            col_buf, col_buf, line(2), line(3),
-            col_buf, col_buf, line(2), line(3),
-            dma(4, tiles), dma(5, tiles), dma(2, routes), dma(2, routes), dma(2, routes), dma(2, routes), dma(2, routes),
+            vmem(4, rows, LANES), pack_buf, pack_buf, vmem(2, rows, LANES), line(3), line(2),
+            line(3), line(2), corner_buf, corner_buf, line(2), line(3), line(2), line(3),
+            pltpu.SMEM((n_sub, 2), F32),
+            dma(4, tiles), dma(5, tiles), pltpu.SemaphoreType.DMA,
+            dma(3, 2, 4), dma(2, 2, 4), dma(3, 2, 4), dma(2, routes), dma(2, 4), dma(3, 2, 2 * tiles), dma(2, 2),
         ],
         compiler_params=pltpu.CompilerParams(
             collective_id=0, has_side_effects=True, vmem_limit_bytes=31 * MIB

time: 98.5 us -> 81.4 us (0.83)
  Pallas kernels: 96.2 us -> 79.3 us
    pallas_call x1, Pallas kernels: 79.2 us -> 66.7 us  [local_step(): front_call(vel_u, vel_v, temperature, salinity, sea_level, trans_u, trans...]
    pallas_call x1, Pallas kernels: 17 us -> 12.6 us  [local_step(): return tuple(back_call(*shared))]
where the time goes in v2:
time: 81.4 us; the launch traced here: 81.3 us
  Pallas kernels  79.3 us (97%)
  local copies, waits for them, and re-layouts  1.37 us (2%)
    pallas_call x1, Pallas kernels, local_step(): front_call(vel_u, vel_v, temperature, salinity, sea_level, trans_u, trans...  66.7 us
    pallas_call x1, Pallas kernels, local_step(): return tuple(back_call(*shared))  12.6 us

profile of v2, /device:TPU:0, one launch (start us, length us, event | category | flops | bytes accessed | tf_op | source)
XLA Modules:
  0.0 81.3 jit_solution(5483923848406904885)
XLA Ops:
  0.6 1.4 %copy.17.tide_hbm = f32[30,2]{1,0:T(8,128)} copy(f32[30,2]{0,1:T(2,128)} %param.19) | data formatting | bytes 480 | tf_op args[9]
  2.0 66.7 %front.1 = (f32[5,31,80,128]{3,2,1,0:T(8,128)S(1)}, f32[5,31,80,128]{3,2,1,0:T(8,128)S(1)}, f32[5,31,80,128]{3,2,1,0:T(8,128)S(1)}, f32[5,31,80,128]{3,2,1,0:T(8...) custom-call(f32[31,64,512]{2,1,0:T(8,128)} %u_hbm.1, ...), custom_call_target="tpu_custom_call" | custom-call | tf_op jit(solution)/shard_map/front/pallas_call | solution.py:743
  68.7 12.6 %back.1 = (f32[64,512]{1,0:T(8,128)}, f32[64,512]{1,0:T(8,128)}, f32[64,512]{1,0:T(8,128)}, f32[31,64,512]{2,1,0:T(8,128)}, f32[31,64,512]{2,1,0:T(8,128)}, /*in...) custom-call(f32[5,31,80,128]{3,2,1,0:T(8,128)S(1)} %get-tuple-element.14.us, f32[5,31,80,128]{3,2,1,0:T(8,128)S(1)} %get-tuple-element.15.vs, ...), custom_call_target="tpu_custom_call" | custom-call | tf_op jit(solution)/shard_map/back/pallas_call | solution.py:746

commit v3 on v2

--- a/solution.py
+++ b/solution.py
@@ -24,11 +24,11 @@
 COMPASS = (NORTH, SOUTH, EAST, WEST, NORTH_EAST, NORTH_WEST, SOUTH_EAST, SOUTH_WEST)
 SLOT = 32
 BLOCK = 16
-CROSS_ROWS = 72
-FLOW_ROWS = 64
 SOLVE_ROWS = 32
-SUB_ROWS = 16
+SUB_ROWS = 32
 BACK_ROWS = 16
+UNROLL = 2
+EDGE_UNROLL = 3
 MIB = 2**20
 
 
@@ -55,18 +55,40 @@
     def east(parts):
         last = lane_iota(parts[0].shape[0]) == LANES - 1
         moved = [roll(x, LANES - 1) for x in parts]
-        return [jnp.where(last, moved[(c + 1) % ring], moved[c]) for c in range(ring)]
+        return [pick(last, moved[(c + 1) % ring], moved[c]) for c in range(ring)]
 
     def west(parts):
         first = lane_iota(parts[0].shape[0]) == 0
         moved = [roll(x, 1) for x in parts]
-        return [jnp.where(first, moved[(c - 1) % ring], moved[c]) for c in range(ring)]
+        return [pick(first, moved[(c - 1) % ring], moved[c]) for c in range(ring)]
 
     def split(ref):
         return [ref.at[f] for f in range(ref.shape[0])]
 
     def scaled(factor, x):
         return x if factor == 1.0 else factor * x
+
+    def real(k):
+        return float(k) if isinstance(k, int) else k.astype(F32)
+
+    def over_levels(body, carry, unroll=UNROLL):
+        def trip(i, carry):
+            for j in range(unroll):
+                carry = body(unroll * i + j, carry)
+            return carry
+
+        carry = lax.fori_loop(0, levels // unroll, trip, carry)
+        for k in range(levels - levels % unroll, levels):
+            carry = body(k, carry)
+        return carry
+
+    def pick(condition, x, other):
+        if jnp.ndim(condition) == 0:
+            return jnp.where(condition, x, other)
+        shape = condition.shape
+        x = x if jnp.ndim(x) else jnp.full(shape, x, F32)
+        other = other if jnp.ndim(other) else jnp.full(shape, other, F32)
+        return lax.select(condition, x, other)
 
     def blank():
         return jnp.zeros((rows, LANES), F32)
@@ -103,8 +125,8 @@
         slot = lane_iota(rows) // HALO
         last, first = blank(), blank()
         for f, ref in enumerate(maps):
-            last = jnp.where(slot == f, roll(ref[tiles - 1, own, :], (HALO * f + HALO) % LANES), last)
-            first = jnp.where(slot == f, roll(ref[0, own, :], HALO * f), first)
+            last = pick(slot == f, roll(ref[tiles - 1, own, :], (HALO * f + HALO) % LANES), last)
+            first = pick(slot == f, roll(ref[0, own, :], HALO * f), first)
         pack_east[...] = last
         pack_west[...] = first
 
@@ -138,7 +160,7 @@
         for f, ref in enumerate(maps):
             e = roll(from_east[here, :], (LANES - HALO * f) % LANES)
             w = roll(from_west[here, :], LANES - HALO - HALO * f)
-            ref[halo_tile, pl.ds(start, n), :] = jnp.where(easterly, e, w)
+            ref[halo_tile, pl.ds(start, n), :] = pick(easterly, e, w)
 
     def front(
         u_hbm, v_hbm, t_hbm, s_hbm, eta_hbm, tu_hbm, tv_hbm, depth_hbm, kmt_hbm, tide_hbm,
@@ -162,6 +184,8 @@
         rim_w1, rim_w2, rim_w3 = split(rim_w)
         zero = blank()
         lane = lane_iota(rows)
+        low_half = lane < LANES // 2
+        pair_of_lane, odd = lane // 2, lane % 2 == 1
 
         barrier = pltpu.get_barrier_semaphore()
         for way in COMPASS:
@@ -228,17 +252,51 @@
 
             def level(k, total):
                 half = (rho_s * sm[c, k, body_rows, :] - rho_t * tm[c, k, body_rows, :]) + rho_0
-                half = jnp.where(k.astype(F32) < k_cell, half, zero)
+                half = pick(real(k) < k_cell, half, zero)
                 middle = total + half
                 p[c, k, body_rows, :] = scale * middle
                 return middle + half
 
-            lax.fori_loop(0, levels, level, zero)
+            over_levels(level, zero)
             return _
 
-        for c in range(tiles):
-            wait_all([tracer_load[c], tracer_load[tiles + c]])
-            pressure_tile(c, 0)
+        wait_all(tracer_load)
+        lax.fori_loop(0, tiles, pressure_tile, 0)
+
+        def tracer_tile(c, _):
+            k_cell = k_map[c, own, :]
+            dz = depth_map[c, own, :] / jnp.maximum(k_cell, 1.0)
+            safe = pick(k_cell > 0, dz, 1.0)
+            couple = (TIME_STEP * DIFF_KT) / (safe * safe)
+
+            def down(k, carry):
+                lower, keep, part_t, part_s = carry
+                kf = real(k)
+                wet = kf < k_cell
+                upper = pick(kf + 1.0 < k_cell, couple, zero)
+                turn = 1.0 + lower * keep
+                inv = 1.0 / (turn + upper)
+                gain_a[k] = upper * inv
+                part_t = (pick(wet, tm[c, k, body_rows, :], zero) + lower * part_t) * inv
+                part_s = (pick(wet, sm[c, k, body_rows, :], zero) + lower * part_s) * inv
+                tm[c, k, body_rows, :] = part_t
+                sm[c, k, body_rows, :] = part_s
+                return upper, turn * inv, part_t, part_s
+
+            over_levels(down, (zero, zero, zero, zero))
+
+            def up(i, carry):
+                below_t, below_s = carry
+                k = levels - 1 - i
+                gain = gain_a[k]
+                below_t = tm[c, k, body_rows, :] + gain * below_t
+                below_s = sm[c, k, body_rows, :] + gain * below_s
+                tm[c, k, body_rows, :] = below_t
+                sm[c, k, body_rows, :] = below_s
+                return below_t, below_s
+
+            over_levels(up, (zero, zero))
+            return _
 
         def edges(columns, top_rows, bottom_rows):
             def level(k, packed):
@@ -247,8 +305,8 @@
                 for pair, acc in zip(columns, packed):
                     for f, ref in pair:
                         slot = SLOT * f + k
-                        both = jnp.where(lane < LANES // 2, ref[0, k, body_rows, :], ref[tiles - 1, k, body_rows, :])
-                        acc = jnp.where(lane // 2 == slot, roll(both, 2 * slot + 1), acc)
+                        both = pick(low_half, ref[0, k, body_rows, :], ref[tiles - 1, k, body_rows, :])
+                        acc = pick(pair_of_lane == slot, roll(both, 2 * slot + 1), acc)
                     out.append(acc)
                 for c in range(tiles):
                     for ref, dst in top_rows:
@@ -257,7 +315,7 @@
                         dst[c, row, :] = ref[c, k, pl.ds(PAD + rows - 1, 1), :]
                 return tuple(out)
 
-            return lax.fori_loop(0, levels, level, (zero,) * len(columns))
+            return over_levels(level, (zero,) * len(columns), EDGE_UNROLL)
 
         wait_all(flow_load)
         cols_uv, cols_p, cols_ts, cols_us = split(cols)
@@ -290,41 +348,6 @@
         far += column_rims(pk_e2, pk_w2, rim_w2, rim_e2, baro_cols)
         far += corner_rims(pk_e2, pk_w2, rim_w2, rim_e2, baro_corners, HALO)
         start_all(far)
-
-        def tracer_tile(c, _):
-            k_cell = k_map[c, own, :]
-            dz = depth_map[c, own, :] / jnp.maximum(k_cell, 1.0)
-            safe = jnp.where(k_cell > 0, dz, 1.0)
-            couple = (TIME_STEP * DIFF_KT) / (safe * safe)
-
-            def down(k, carry):
-                lower, keep, part_t, part_s = carry
-                kf = k.astype(F32)
-                wet = kf < k_cell
-                upper = jnp.where(kf + 1.0 < k_cell, couple, zero)
-                turn = 1.0 + lower * keep
-                inv = 1.0 / (turn + upper)
-                gain_a[k] = upper * inv
-                part_t = (jnp.where(wet, tm[c, k, body_rows, :], zero) + lower * part_t) * inv
-                part_s = (jnp.where(wet, sm[c, k, body_rows, :], zero) + lower * part_s) * inv
-                tm[c, k, body_rows, :] = part_t
-                sm[c, k, body_rows, :] = part_s
-                return upper, turn * inv, part_t, part_s
-
-            lax.fori_loop(0, levels, down, (zero, zero, zero, zero))
-
-            def up(i, carry):
-                below_t, below_s = carry
-                k = levels - 1 - i
-                gain = gain_a[k]
-                below_t = tm[c, k, body_rows, :] + gain * below_t
-                below_s = sm[c, k, body_rows, :] + gain * below_s
-                tm[c, k, body_rows, :] = below_t
-                sm[c, k, body_rows, :] = below_s
-                return below_t, below_s
-
-            lax.fori_loop(0, levels, up, (zero, zero))
-            return _
 
         lax.fori_loop(0, tiles, tracer_tile, 0)
         fr_t4, fr_s4 = split(first_row4)
@@ -371,7 +394,7 @@
                 kv_map[c, here, :] = k_v
                 dzu_map[c, here, :] = dz_u
                 dzv_map[c, here, :] = dz_v
-                wet_map[c, here, :] = jnp.where(k_cell[c] > 0, dt_sub, 0.0)
+                wet_map[c, here, :] = pick(k_cell[c] > 0, dt_sub, 0.0)
                 hu_map[c, here, :] = dt_sub * (k_u * dz_u)
                 hv_map[c, here, :] = dt_sub * (k_v * dz_v)
 
@@ -391,17 +414,17 @@
                 k_face = count[c, own, :]
 
                 def level(k, done, ref=ref, k_face=k_face):
-                    ref[c, k, body_rows, :] = jnp.where(k.astype(F32) < k_face, ref[c, k, body_rows, :], zero)
+                    ref[c, k, body_rows, :] = pick(real(k) < k_face, ref[c, k, body_rows, :], zero)
                     return done
 
-                lax.fori_loop(0, levels, level, 0)
+                over_levels(level, 0)
             return _
 
         lax.fori_loop(0, tiles, mask_tile, 0)
 
         def fill(columns, norths, souths):
             def masked(x, k, count, tile, here):
-                return x if count is None else jnp.where(k.astype(F32) < count[tile, here, :], x, 0.0)
+                return x if count is None else pick(real(k) < count[tile, here, :], x, 0.0)
 
             def level(k, _):
                 for ref, f, src, count in columns:
@@ -417,12 +440,11 @@
                         ref[c, k, pl.ds(PAD - 1, 1), :] = x
                 return _
 
-            lax.fori_loop(0, levels, level, 0)
-
-        odd = lane % 2 == 1
+            over_levels(level, 0, EDGE_UNROLL)
+
         in_uv, in_ts = split(cols_in)
         wait_all(ex_uvp)
-        in_uv[...] = jnp.where(odd, east_uv[...], west_uv[...])
+        in_uv[...] = pick(odd, east_uv[...], west_uv[...])
         rn_u, rn_v, rn_p = split(row_n)
         rs_u, rs_v = split(row_s)
         fill(
@@ -432,45 +454,43 @@
         )
 
         def corners(k, _):
-            kf = k.astype(F32)
+            kf = real(k)
             x = roll(corner_nw[...], LANES - 1 - 2 * k)
-            u[halo_tile, k, pl.ds(PAD + rows, PAD), :] = jnp.where(kf < ku_map[halo_tile, pl.ds(top, PAD), :], x, 0.0)
+            u[halo_tile, k, pl.ds(PAD + rows, PAD), :] = pick(kf < ku_map[halo_tile, pl.ds(top, PAD), :], x, 0.0)
             x = roll(corner_se[...], LANES - 1 - 2 * (SLOT + k))
-            v[halo_tile, k, pl.ds(0, PAD), :] = jnp.where(kf < kv_map[halo_tile, pl.ds(core - PAD, PAD), :], x, 0.0)
+            v[halo_tile, k, pl.ds(0, PAD), :] = pick(kf < kv_map[halo_tile, pl.ds(core - PAD, PAD), :], x, 0.0)
             return _
 
-        lax.fori_loop(0, levels, corners, 0)
+        over_levels(corners, 0, EDGE_UNROLL)
 
         quarter = 0.25 * TIME_STEP
 
         def momentum(k, _):
-            for r in range(0, PAD + rows, CROSS_ROWS):
-                here, north = pl.ds(r, CROSS_ROWS), pl.ds(r + 1, CROSS_ROWS)
-                vv = [v[c, k, here, :] for c in range(ring)]
-                v_east = east(vv)
-                for c in range(ring):
-                    cross[c, here, :] = (vv[c] + v_east[c]) * (u[c, k, here, :] + u[c, k, north, :])
-            for r in range(PAD, PAD + rows, FLOW_ROWS):
-                here, north, south = pl.ds(r, FLOW_ROWS), pl.ds(r + 1, FLOW_ROWS), pl.ds(r - 1, FLOW_ROWS)
-                uu = [u[c, k, here, :] for c in range(ring)]
-                square = [x + y for x, y in zip(uu, east(uu))]
-                square = [x * x for x in square]
-                square_west = west(square)
-                xx = [cross[c, here, :] for c in range(ring)]
-                x_west = west(xx)
-                pp = [p[c, k, here, :] for c in range(ring)]
-                p_east = east(pp)
-                for c in range(tiles):
-                    push = (square[c] - square_west[c]) + (xx[c] - cross[c, south, :])
-                    us[c, k, here, :] = uu[c] - (scaled(quarter, push) + (p_east[c] - pp[c]))
-                    vv = v[c, k, here, :]
-                    b_here = vv + v[c, k, north, :]
-                    b_south = vv + v[c, k, south, :]
-                    push = (b_here * b_here - b_south * b_south) + (xx[c] - x_west[c])
-                    vs[c, k, here, :] = vv - (scaled(quarter, push) + (p[c, k, north, :] - pp[c]))
+            tall, tall_north = pl.ds(0, PAD + rows), pl.ds(1, PAD + rows)
+            here, north, south = body_rows, pl.ds(PAD + 1, rows), pl.ds(PAD - 1, rows)
+            vv = [v[c, k, tall, :] for c in range(ring)]
+            v_east = east(vv)
+            for c in range(ring):
+                cross[c, tall, :] = (vv[c] + v_east[c]) * (u[c, k, tall, :] + u[c, k, tall_north, :])
+            uu = [u[c, k, here, :] for c in range(ring)]
+            pp = [p[c, k, here, :] for c in range(ring)]
+            centre = [x + y for x, y in zip(uu, west(uu))]
+            centre = [scaled(quarter, x * x) + y for x, y in zip(centre, pp)]
+            centre_east = east(centre)
+            xx = [cross[c, here, :] for c in range(ring)]
+            x_west = west(xx)
+            for c in range(tiles):
+                us[c, k, here, :] = uu[c] - (
+                    (centre_east[c] - centre[c]) + scaled(quarter, xx[c] - cross[c, south, :])
+                )
+                vv = v[c, k, here, :]
+                b_here = vv + v[c, k, north, :]
+                b_south = vv + v[c, k, south, :]
+                push = (b_here * b_here - b_south * b_south) + (xx[c] - x_west[c])
+                vs[c, k, here, :] = vv - (scaled(quarter, push) + (p[c, k, north, :] - pp[c]))
             return _
 
-        lax.fori_loop(0, levels, momentum, 0)
+        over_levels(momentum, 0)
 
         nil = jnp.zeros((SOLVE_ROWS, LANES), F32)
         parts = rows // SOLVE_ROWS
@@ -481,25 +501,25 @@
             faces = []
             for count, dz in ((ku_map, dzu_map), (kv_map, dzv_map)):
                 k_face = count[c, flat, :]
-                safe = jnp.where(k_face > 0, dz[c, flat, :], 1.0)
+                safe = pick(k_face > 0, dz[c, flat, :], 1.0)
                 faces.append((k_face, (TIME_STEP * VISC_KV) / (safe * safe)))
 
             def down(k, carry):
-                kf = k.astype(F32)
+                kf = real(k)
                 out = []
                 for face, ref, gain, state in zip(faces, (us, vs), (gain_a, gain_b), carry):
                     k_face, couple = face
                     lower, keep, part = state
-                    upper = jnp.where(kf + 1.0 < k_face, couple, nil)
+                    upper = pick(kf + 1.0 < k_face, couple, nil)
                     turn = 1.0 + lower * keep
                     inv = 1.0 / (turn + upper)
                     gain[k, pl.ds(0, SOLVE_ROWS), :] = upper * inv
-                    part = (jnp.where(kf < k_face, ref[c, k, here, :], nil) + lower * part) * inv
+                    part = (pick(kf < k_face, ref[c, k, here, :], nil) + lower * part) * inv
                     ref[c, k, here, :] = part
                     out.append((upper, turn * inv, part))
                 return tuple(out)
 
-            lax.fori_loop(0, levels, down, ((nil,) * 3,) * 2)
+            over_levels(down, ((nil,) * 3,) * 2)
 
             def up(j, carry):
                 k = levels - 1 - j
@@ -511,38 +531,48 @@
                     out.append((below, total + below, change + (below - old[c, k, here, :])))
                 return tuple(out)
 
-            sums = lax.fori_loop(0, levels, up, ((nil,) * 3,) * 2)
+            sums = over_levels(up, ((nil,) * 3,) * 2)
             for dz, total_map, force_map, state in zip((dzu_map, dzv_map), (su_map, sv_map), (fu_map, fv_map), sums):
                 _, total, change = state
                 total_map[c, flat, :] = dz[c, flat, :] * total
                 force_map[c, flat, :] = dz[c, flat, :] * change * (1.0 / TIME_STEP)
 
         force_rows, force_cols, force_corners = split(sem_force)
-        ex3 = []
-        for step, c in enumerate((0, tiles - 1) + tuple(range(1, tiles - 1))):
-            lax.fori_loop(0, parts, lambda i, _: (solve_part(c, i), _)[1], 0)
-            low, high, every = pl.ds(core, HALO), pl.ds(top - HALO, HALO), pl.ds(0, 2)
-            sent = remote(
-                force_rows.at[pl.ds(0, 2), pl.ds(2 * step, 2)],
-                (force.at[every, c, high, :], force.at[every, c, pl.ds(PAD, HALO), :], NORTH),
-                (force.at[every, c, low, :], force.at[every, c, pl.ds(top, HALO), :], SOUTH),
-            )
-            if step == 1:
-                rim_pack((fu_map, fv_map), pk_e3, pk_w3)
-                sent += column_rims(pk_e3, pk_w3, rim_w3, rim_e3, force_cols)
-                sent += corner_rims(pk_e3, pk_w3, rim_w3, rim_e3, force_corners, HALO)
-            start_all(sent)
-            ex3 += sent
+        low, high, both = pl.ds(core, HALO), pl.ds(top - HALO, HALO), pl.ds(0, 2)
+
+        def solve_tiles(first, step):
+            def work(i, done):
+                solve_part(first + step * (i // parts), i % parts)
+                return done
+
+            lax.fori_loop(0, 2 * parts, work, 0)
+            sent = []
+            for c in (first, first + step):
+                sent += remote(
+                    force_rows.at[both, pl.ds(2 * c, 2)],
+                    (force.at[both, c, high, :], force.at[both, c, pl.ds(PAD, HALO), :], NORTH),
+                    (force.at[both, c, low, :], force.at[both, c, pl.ds(top, HALO), :], SOUTH),
+                )
+            return sent
+
+        ex3 = solve_tiles(0, tiles - 1)
+        rim_pack((fu_map, fv_map), pk_e3, pk_w3)
+        ex3 += column_rims(pk_e3, pk_w3, rim_w3, rim_e3, force_cols)
+        ex3 += corner_rims(pk_e3, pk_w3, rim_w3, rim_e3, force_corners, HALO)
+        start_all(ex3)
+        late = solve_tiles(1, 1)
+        start_all(late)
+        ex3 += late
 
         (packed,) = edges((((0, us),),), (), ((vs, lr_v4),))
-        cols_us[...] = jnp.where(lane // 2 == levels, roll(su_map[tiles - 1, own, :], 2 * levels + 1), packed)
+        cols_us[...] = pick(pair_of_lane == levels, roll(su_map[tiles - 1, own, :], 2 * levels + 1), packed)
         for c in range(tiles):
             lr_v4[c, pl.ds(levels, 1), :] = sv_map[c, pl.ds(top - 1, 1), :]
         ex_star = remote(sem_star, (cols_us, west_us, EAST), (lr_v4, rs_v4, NORTH))
         start_all(ex_star)
 
         wait_all(ex_ts)
-        in_ts[...] = jnp.where(odd, east_ts[...], west_ts[...])
+        in_ts[...] = pick(odd, east_ts[...], west_ts[...])
         fill(
             ((tm, 0, in_ts, None), (sm, 1, in_ts, None)),
             ((tm, rn_t4, None), (sm, rn_s4, None)),
@@ -565,7 +595,7 @@
             here = pl.ds(start, n)
             for ref, count in ((eta_map, k_out), (tu_map, ku_map), (tv_map, kv_map)):
                 for c in range(ring):
-                    ref[c, here, :] = jnp.where(count[c, here, :] > 0, ref[c, here, :], 0.0)
+                    ref[c, here, :] = pick(count[c, here, :] > 0, ref[c, here, :], 0.0)
 
         in_blocks(start_fields, PAD, full_n)
         tide_load.wait()
@@ -577,26 +607,28 @@
             here = pl.ds(start, n)
             for ref, count in ((fu_map, ku_map), (fv_map, kv_map)):
                 for c in range(ring):
-                    ref[c, here, :] = jnp.where(count[c, here, :] > 0, dt_sub * ref[c, here, :], 0.0)
+                    ref[c, here, :] = pick(count[c, here, :] > 0, dt_sub * ref[c, here, :], 0.0)
 
         in_blocks(force_fields, PAD, full_n)
 
         def subcycle(low, high):
+            chunks = [(r, min(SUB_ROWS, high - r)) for r in range(low, high, SUB_ROWS)]
+
             def body(n, _):
-                tide_u, tide_v = tide[n, 0], tide[n, 1]
+                tide_u, tide_v = tide[0, n], tide[1, n]
                 weight = weight_norm * ((n + 1) * (n_sub - n)).astype(F32)
-                for r in range(low, high, SUB_ROWS):
-                    here, south = pl.ds(r, SUB_ROWS), pl.ds(r - 1, SUB_ROWS)
+                for r, n_r in chunks:
+                    here, south = pl.ds(r, n_r), pl.ds(r - 1, n_r)
                     tu = [tu_map[c, here, :] for c in range(ring)]
                     tu_west = west(tu)
                     for c in range(ring):
                         spread = (tu[c] - tu_west[c]) + (tv_map[c, here, :] - tv_map[c, south, :])
                         eta_map[c, here, :] = eta_map[c, here, :] - wet_map[c, here, :] * spread
-                for r in range(low, high, SUB_ROWS):
-                    here, north = pl.ds(r, SUB_ROWS), pl.ds(r + 1, SUB_ROWS)
+                for r, n_r in chunks:
+                    here, north = pl.ds(r, n_r), pl.ds(r + 1, n_r)
                     eta = [eta_map[c, here, :] for c in range(ring)]
                     eta_east = east(eta)
-                    averaged = r + SUB_ROWS > core - 1 and r < top
+                    averaged = r + n_r > core - 1 and r < top
                     for c in range(ring):
                         drive = hu_map[c, here, :] * (tide_u - scaled(GRAVITY, eta_east[c] - eta[c]))
                         tu = tu_map[c, here, :] + (drive + fu_map[c, here, :])
@@ -636,7 +668,7 @@
         ):
             for c in range(n):
                 depth = count[c, here, :] * dz[c, here, :]
-                safe = jnp.where(depth > 0, depth, 1.0)
+                safe = pick(depth > 0, depth, 1.0)
                 out[c, here, :] = (mean_map[c, here, :] - total_map[c, here, :]) / safe
 
     group = 4
@@ -657,7 +689,7 @@
                 here, north = pl.ds(r, PAD), pl.ds(r + 1, PAD)
                 flat = pl.ds(r + core - PAD, PAD)
                 for c in range(tiles):
-                    vv = jnp.where(kf < kv_map[c, flat, :], vs[c, k, here, :] + cv_map[c, flat, :], 0.0)
+                    vv = pick(kf < kv_map[c, flat, :], vs[c, k, here, :] + cv_map[c, flat, :], 0.0)
                     if r >= PAD:
                         v_o[i, pl.ds(r - PAD, PAD), pl.ds(c * LANES, LANES)] = vv
                     vv = half * vv
@@ -669,7 +701,7 @@
                 out_rows = pl.ds(r - PAD, BACK_ROWS)
                 uu = []
                 for c in range(ring):
-                    x = jnp.where(kf < ku_map[c, flat, :], us[c, k, here, :] + cu_map[c, flat, :], 0.0)
+                    x = pick(kf < ku_map[c, flat, :], us[c, k, here, :] + cu_map[c, flat, :], 0.0)
                     if c < tiles:
                         u_o[i, out_rows, pl.ds(c * LANES, LANES)] = x
                     uu.append(half * x)
@@ -679,11 +711,12 @@
                     fx_west = west(fx)
                     for c in range(tiles):
                         spread = (fx[c] - fx_west[c]) + (store[c, here, :] - store[c, south, :])
-                        new = jnp.where(kf < k_map[c, flat, :], tt[c] - spread, 0.0)
+                        new = pick(kf < k_map[c, flat, :], tt[c] - spread, 0.0)
                         out[i, out_rows, pl.ds(c * LANES, LANES)] = new
             return _
 
-        lax.fori_loop(0, group, level, 0)
+        for i in range(group):
+            level(i, 0)
 
     vmem = lambda *shape: pltpu.VMEM(shape, F32)
     flat = lambda n: vmem(n, ring, flat_rows, LANES)
@@ -694,7 +727,7 @@
     rim_buf = vmem(3, rows + 2 * HALO, LANES)
     col_buf, corner_buf = vmem(rows, LANES), vmem(PAD, LANES)
     dma = lambda *shape: pltpu.SemaphoreType.DMA(shape)
-    shared = [cube_buf, cube_buf, cube_buf, cube_buf, vmem(3, tiles, rows, LANES), flat(2), flat(3)]
+    shared = [cube_buf, vmem(tiles, levels, ext_rows, LANES), cube_buf, cube_buf, vmem(3, tiles, rows, LANES), flat(2), flat(3)]
     routes = 7
     any_spec = pl.BlockSpec(memory_space=pl.ANY)
     vmem_spec = pl.BlockSpec(memory_space=pltpu.VMEM)
@@ -705,18 +738,18 @@
         in_specs=[any_spec] * 10,
         out_specs=[vmem_spec] * len(shared),
         scratch_shapes=[
-            cube_buf, cube_buf, cube_buf, gain_buf, gain_buf,
+            cube_buf, cube_buf, cube_buf, gain_buf, vmem(levels, SOLVE_ROWS, LANES),
             vmem(ring, ext_rows, LANES), pltpu.VMEM((tiles, rows, LANES), jnp.int32),
             flat(2), flat(3), flat(3), flat(2), flat(3), flat(2), flat(2),
             pack_buf, pack_buf, rim_buf, rim_buf,
             vmem(4, rows, LANES), pack_buf, pack_buf, vmem(2, rows, LANES), line(3), line(2),
             line(3), line(2), corner_buf, corner_buf, line(2), line(3), line(2), line(3),
-            pltpu.SMEM((n_sub, 2), F32),
+            pltpu.SMEM((2, n_sub), F32),
             dma(4, tiles), dma(5, tiles), pltpu.SemaphoreType.DMA,
             dma(3, 2, 4), dma(2, 2, 4), dma(3, 2, 4), dma(2, routes), dma(2, 4), dma(3, 2, 2 * tiles), dma(2, 2),
         ],
         compiler_params=pltpu.CompilerParams(
-            collective_id=0, has_side_effects=True, vmem_limit_bytes=31 * MIB
+            collective_id=0, has_side_effects=True, vmem_limit_bytes=32 * MIB
         ),
     )
     plane_out = pl.BlockSpec((rows, cols), lambda i: (0, 0))
@@ -741,7 +774,7 @@
         levels, rows, cols = vel_u.shape
         front_call, back_call = kernels(mesh, levels, rows, cols, tide_force.shape[0])
         shared = front_call(
-            vel_u, vel_v, temperature, salinity, sea_level, trans_u, trans_v, bathymetry, kmt_levels, tide_force
+            vel_u, vel_v, temperature, salinity, sea_level, trans_u, trans_v, bathymetry, kmt_levels, tide_force.T
         )
         return tuple(back_call(*shared))
 

time: 81.4 us -> 74.5 us (0.915)
  Pallas kernels: 79.3 us -> 73.5 us
  local copies, waits for them, and re-layouts: 1.37 us -> 0 us
    pallas_call x1, Pallas kernels: 66.7 us -> 52.2 us  [local_step(): front_call(vel_u, vel_v, temperature, salinity, sea_level, trans_u, trans...]
    pallas_call x1, Pallas kernels: 12.6 us -> 21.3 us  [local_step(): return tuple(back_call(*shared))]
    unnamed x1 -> x0, local copies, waits for them, and re-layouts: 1.37 us -> none
where the time goes in v3:
time: 74.5 us; the launch traced here: 74.2 us
  Pallas kernels  73.5 us (99%)
    pallas_call x1, Pallas kernels, local_step(): front_call(vel_u, vel_v, temperature, salinity, sea_level, trans_u, trans...  52.2 us
    pallas_call x1, Pallas kernels, local_step(): return tuple(back_call(*shared))  21.3 us

profile of v3, /device:TPU:0, one launch (start us, length us, event | category | flops | bytes accessed | tf_op | source)
XLA Modules:
  0.0 74.2 jit_solution(7138319767185564515)
XLA Ops:
  0.6 52.2 %front.1 = (f32[5,31,80,128]{3,2,1,0:T(8,128)S(1)}, f32[4,31,80,128]{3,2,1,0:T(8,128)S(1)}, f32[5,31,80,128]{3,2,1,0:T(8,128)S(1)}, f32[5,31,80,128]{3,2,1,0:T(8...) custom-call(f32[31,64,512]{2,1,0:T(8,128)} %u_hbm.1, ...), custom_call_target="tpu_custom_call" | custom-call | tf_op jit(solution)/shard_map/front/pallas_call | solution.py:776
  52.9 21.3 %back.1 = (f32[64,512]{1,0:T(8,128)}, f32[64,512]{1,0:T(8,128)}, f32[64,512]{1,0:T(8,128)}, f32[31,64,512]{2,1,0:T(8,128)}, f32[31,64,512]{2,1,0:T(8,128)}, /*in...) custom-call(f32[5,31,80,128]{3,2,1,0:T(8,128)S(1)} %get-tuple-element.14.us, f32[4,31,80,128]{3,2,1,0:T(8,128)S(1)} %get-tuple-element.15.vs, ...), custom_call_target="tpu_custom_call" | custom-call | tf_op jit(solution)/shard_map/back/pallas_call | solution.py:779

commit v4 on v3

--- a/solution.py
+++ b/solution.py
@@ -168,7 +168,7 @@
         u, v, p, gain_a, gain_b, cross, kmt_int, geo, thick, baro, force, coef, mean, depth_sum,
         pk_e, pk_w, rim_w, rim_e, cols, cols_e, cols_w, cols_in, first_row, last_row,
         row_n, row_s, corner_nw, corner_se, first_row4, last_row4, row_n4, row_s4, tide,
-        load_sems, plane_sems, tide_sem, sem_near, sem_far, sem_baro, sem_uvp, sem_ts, sem_force, sem_star,
+        load_sems, plane_sems, tide_sem, sem_near, sem_far, sem_baro, sem_uv, sem_p, sem_ts, sem_force, sem_star,
     ):
         k_map, depth_map = split(geo)
         eta_map, tu_map, tv_map = split(baro)
@@ -218,8 +218,8 @@
         flow_load = cube_load(sem_u, u_hbm, u) + cube_load(sem_v, v_hbm, v)
         tide_load = pltpu.make_async_copy(tide_hbm, tide, tide_sem)
         start_all(geo_load)
+        start_all(flow_load)
         start_all(tracer_load)
-        start_all(flow_load)
         start_all(baro_load)
         tide_load.start()
 
@@ -242,26 +242,6 @@
         near += column_rims(pk_e1, pk_w1, rim_w1, rim_e1, near_cols)
         near += corner_rims(pk_e1, pk_w1, rim_w1, rim_e1, near_corners, NEAR)
         start_all(near)
-
-        rho_s, rho_t = 0.5 * BETA_S, 0.5 * ALPHA_T
-        rho_0 = rho_t * T_REF - rho_s * S_REF
-
-        def pressure_tile(c, _):
-            k_cell = k_map[c, own, :]
-            scale = (TIME_STEP * GRAVITY) * (depth_map[c, own, :] / jnp.maximum(k_cell, 1.0))
-
-            def level(k, total):
-                half = (rho_s * sm[c, k, body_rows, :] - rho_t * tm[c, k, body_rows, :]) + rho_0
-                half = pick(real(k) < k_cell, half, zero)
-                middle = total + half
-                p[c, k, body_rows, :] = scale * middle
-                return middle + half
-
-            over_levels(level, zero)
-            return _
-
-        wait_all(tracer_load)
-        lax.fori_loop(0, tiles, pressure_tile, 0)
 
         def tracer_tile(c, _):
             k_cell = k_map[c, own, :]
@@ -323,20 +303,46 @@
         west_uv, west_ts, west_us = split(cols_w)
         fr_u, fr_v, fr_p = split(first_row)
         lr_u, lr_v = split(last_row)
-        cols_uv[...], cols_p[...] = edges(
-            (((0, u), (1, v)), ((0, p),)), ((u, fr_u), (v, fr_v), (p, fr_p)), ((u, lr_u), (v, lr_v))
-        )
-        ex_uvp = remote(
-            sem_uvp,
+        rn_u, rn_v, rn_p = split(row_n)
+        rs_u, rs_v = split(row_s)
+        (packed,) = edges((((0, u), (1, v)),), ((u, fr_u), (v, fr_v)), ((u, lr_u), (v, lr_v)))
+        cols_uv[...] = packed
+        two = pl.ds(0, 2)
+        ex_uv = remote(
+            sem_uv,
+            (first_row.at[two], row_n.at[two], SOUTH),
+            (last_row, row_s, NORTH),
             (cols_uv, east_uv, WEST),
-            (cols_p, east_p, WEST),
             (cols_uv, west_uv, EAST),
-            (first_row, row_n, SOUTH),
-            (last_row, row_s, NORTH),
             (cols_uv.at[pl.ds(0, PAD), :], corner_nw, SOUTH_EAST),
             (cols_uv.at[pl.ds(rows - PAD, PAD), :], corner_se, NORTH_WEST),
         )
-        start_all(ex_uvp)
+        start_all(ex_uv)
+
+        rho_s, rho_t = 0.5 * BETA_S, 0.5 * ALPHA_T
+        rho_0 = rho_t * T_REF - rho_s * S_REF
+
+        def pressure_tile(c, _):
+            k_cell = k_map[c, own, :]
+            scale = (TIME_STEP * GRAVITY) * (depth_map[c, own, :] / jnp.maximum(k_cell, 1.0))
+
+            def level(k, total):
+                half = (rho_s * sm[c, k, body_rows, :] - rho_t * tm[c, k, body_rows, :]) + rho_0
+                half = pick(real(k) < k_cell, half, zero)
+                middle = total + half
+                p[c, k, body_rows, :] = scale * middle
+                return middle + half
+
+            over_levels(level, zero)
+            return _
+
+        wait_all(tracer_load)
+        lax.fori_loop(0, tiles, pressure_tile, 0)
+
+        (packed,) = edges((((0, p),),), ((p, fr_p),), ())
+        cols_p[...] = packed
+        ex_p = remote(sem_p, (fr_p, rn_p, SOUTH), (cols_p, east_p, WEST))
+        start_all(ex_p)
 
         wait_all(baro_load)
         rim_pack((eta_map, tu_map, tv_map), pk_e2, pk_w2)
@@ -356,7 +362,6 @@
         rs_t4, rs_s4, rs_v4 = split(row_s4)
         (packed,) = edges((((0, tm), (1, sm)),), ((tm, fr_t4), (sm, fr_s4)), ((tm, lr_t4), (sm, lr_s4)))
         cols_ts[...] = packed
-        two = pl.ds(0, 2)
         ex_ts = remote(
             sem_ts,
             (cols_ts, east_ts, WEST),
@@ -443,10 +448,9 @@
             over_levels(level, 0, EDGE_UNROLL)
 
         in_uv, in_ts = split(cols_in)
-        wait_all(ex_uvp)
+        wait_all(ex_uv)
+        wait_all(ex_p)
         in_uv[...] = pick(odd, east_uv[...], west_uv[...])
-        rn_u, rn_v, rn_p = split(row_n)
-        rs_u, rs_v = split(row_s)
         fill(
             ((u, 0, in_uv, ku_map), (v, 1, in_uv, kv_map), (p, 0, east_p, None)),
             ((u, rn_u, ku_map), (v, rn_v, kv_map), (p, rn_p, None)),
@@ -715,8 +719,7 @@
                         out[i, out_rows, pl.ds(c * LANES, LANES)] = new
             return _
 
-        for i in range(group):
-            level(i, 0)
+        lax.fori_loop(0, group, level, 0)
 
     vmem = lambda *shape: pltpu.VMEM(shape, F32)
     flat = lambda n: vmem(n, ring, flat_rows, LANES)
@@ -728,7 +731,7 @@
     col_buf, corner_buf = vmem(rows, LANES), vmem(PAD, LANES)
     dma = lambda *shape: pltpu.SemaphoreType.DMA(shape)
     shared = [cube_buf, vmem(tiles, levels, ext_rows, LANES), cube_buf, cube_buf, vmem(3, tiles, rows, LANES), flat(2), flat(3)]
-    routes = 7
+    routes = 6
     any_spec = pl.BlockSpec(memory_space=pl.ANY)
     vmem_spec = pl.BlockSpec(memory_space=pltpu.VMEM)
     front_call = pl.pallas_call(
@@ -746,7 +749,7 @@
             line(3), line(2), corner_buf, corner_buf, line(2), line(3), line(2), line(3),
             pltpu.SMEM((2, n_sub), F32),
             dma(4, tiles), dma(5, tiles), pltpu.SemaphoreType.DMA,
-            dma(3, 2, 4), dma(2, 2, 4), dma(3, 2, 4), dma(2, routes), dma(2, 4), dma(3, 2, 2 * tiles), dma(2, 2),
+            dma(3, 2, 4), dma(2, 2, 4), dma(3, 2, 4), dma(2, routes), dma(2, 2), dma(2, 4), dma(3, 2, 2 * tiles), dma(2, 2),
         ],
         compiler_params=pltpu.CompilerParams(
             collective_id=0, has_side_effects=True, vmem_limit_bytes=32 * MIB

time: 74.5 us -> 66.9 us (0.90)
  Pallas kernels: 73.5 us -> 66.1 us
    pallas_call x1, Pallas kernels: 21.3 us -> 12.8 us  [local_step(): return tuple(back_call(*shared))]
    pallas_call x1, Pallas kernels: 52.2 us -> 53.3 us  [local_step(): front_call(vel_u, vel_v, temperature, salinity, sea_level, trans_u, trans...]
where the time goes in v4:
time: 66.9 us; the launch traced here: 66.7 us
  Pallas kernels  66.1 us (99%)
    pallas_call x1, Pallas kernels, local_step(): front_call(vel_u, vel_v, temperature, salinity, sea_level, trans_u, trans...  53.3 us
    pallas_call x1, Pallas kernels, local_step(): return tuple(back_call(*shared))  12.8 us

profile of v4, /device:TPU:0, one launch (start us, length us, event | category | flops | bytes accessed | tf_op | source)
XLA Modules:
  0.0 66.7 jit_solution(3226837820459302999)
XLA Ops:
  0.6 53.3 %front.1 = (f32[5,31,80,128]{3,2,1,0:T(8,128)S(1)}, f32[4,31,80,128]{3,2,1,0:T(8,128)S(1)}, f32[5,31,80,128]{3,2,1,0:T(8,128)S(1)}, f32[5,31,80,128]{3,2,1,0:T(8...) custom-call(f32[31,64,512]{2,1,0:T(8,128)} %u_hbm.1, ...), custom_call_target="tpu_custom_call" | custom-call | tf_op jit(solution)/shard_map/front/pallas_call | solution.py:779
  54.0 12.8 %back.1 = (f32[64,512]{1,0:T(8,128)}, f32[64,512]{1,0:T(8,128)}, f32[64,512]{1,0:T(8,128)}, f32[31,64,512]{2,1,0:T(8,128)}, f32[31,64,512]{2,1,0:T(8,128)}, /*in...) custom-call(f32[5,31,80,128]{3,2,1,0:T(8,128)S(1)} %get-tuple-element.14.us, f32[4,31,80,128]{3,2,1,0:T(8,128)S(1)} %get-tuple-element.15.vs, ...), custom_call_target="tpu_custom_call" | custom-call | tf_op jit(solution)/shard_map/back/pallas_call | solution.py:782

commit v5 on v4

--- a/solution.py
+++ b/solution.py
@@ -26,9 +26,9 @@
 BLOCK = 16
 SOLVE_ROWS = 32
 SUB_ROWS = 32
-BACK_ROWS = 16
 UNROLL = 2
 EDGE_UNROLL = 3
+FLOW_UNROLL = 4
 MIB = 2**20
 
 
@@ -174,7 +174,7 @@
         eta_map, tu_map, tv_map = split(baro)
         dz_map, dzu_map, dzv_map = split(thick)
         k_out, ku_map, kv_map = split(counts)
-        wet_map, hu_map, hv_map = split(coef)
+        hu_map, hv_map = split(coef)
         fu_map, fv_map = split(force)
         mu_map, mv_map = split(mean)
         su_map, sv_map = split(depth_sum)
@@ -196,13 +196,12 @@
                 pltpu.make_async_copy(src.at[:, pl.ds(c * LANES, LANES)], dst(c), sems.at[c]) for c in range(tiles)
             ]
 
+        def cube_tile(sems, src, dst, c):
+            lanes = pl.ds(pl.multiple_of(c * LANES, LANES), LANES)
+            return pltpu.make_async_copy(src.at[:, :, lanes], dst.at[c, :, body_rows, :], sems.at[c])
+
         def cube_load(sems, src, dst):
-            return [
-                pltpu.make_async_copy(
-                    src.at[:, :, pl.ds(c * LANES, LANES)], dst.at[c, :, body_rows, :], sems.at[c]
-                )
-                for c in range(tiles)
-            ]
+            return [cube_tile(sems, src, dst, c) for c in range(tiles)]
 
         sem_k, sem_h, sem_e, sem_tu, sem_tv = split(plane_sems)
         sem_t, sem_s, sem_u, sem_v = split(load_sems)
@@ -214,12 +213,14 @@
             + plane_load(sem_tu, tu_hbm, lambda c: tu_map.at[c, own, :])
             + plane_load(sem_tv, tv_hbm, lambda c: tv_map.at[c, own, :])
         )
-        tracer_load = cube_load(sem_t, t_hbm, tm) + cube_load(sem_s, s_hbm, sm)
+        tracer_load = []
+        for c in range(tiles):
+            tracer_load += [cube_tile(sem_t, t_hbm, tm, c), cube_tile(sem_s, s_hbm, sm, c)]
         flow_load = cube_load(sem_u, u_hbm, u) + cube_load(sem_v, v_hbm, v)
         tide_load = pltpu.make_async_copy(tide_hbm, tide, tide_sem)
         start_all(geo_load)
+        start_all(tracer_load)
         start_all(flow_load)
-        start_all(tracer_load)
         start_all(baro_load)
         tide_load.start()
 
@@ -242,6 +243,24 @@
         near += column_rims(pk_e1, pk_w1, rim_w1, rim_e1, near_cols)
         near += corner_rims(pk_e1, pk_w1, rim_w1, rim_e1, near_corners, NEAR)
         start_all(near)
+
+        rho_s, rho_t = 0.5 * BETA_S, 0.5 * ALPHA_T
+        rho_0 = rho_t * T_REF - rho_s * S_REF
+
+        def pressure_tile(c, _):
+            k_cell = k_map[c, own, :]
+            scale = (TIME_STEP * GRAVITY) * (depth_map[c, own, :] / jnp.maximum(k_cell, 1.0))
+
+            def level(k, total):
+                half = (rho_s * sm[c, k, body_rows, :] - rho_t * tm[c, k, body_rows, :]) + rho_0
+                half = pick(real(k) < k_cell, half, zero)
+                middle = total + half
+                p[c, k, body_rows, :] = scale * middle
+                return middle + half
+
+            over_levels(level, zero)
+            return _
+
 
         def tracer_tile(c, _):
             k_cell = k_map[c, own, :]
@@ -277,6 +296,24 @@
 
             over_levels(up, (zero, zero))
             return _
+
+        def arrived(c):
+            cube_tile(sem_t, t_hbm, tm, c).wait()
+            cube_tile(sem_s, s_hbm, sm, c).wait()
+
+        def both_passes(c, done):
+            arrived(c)
+            pressure_tile(c, 0)
+            tracer_tile(c, 0)
+            return done
+
+        def pressure_pass(c, done):
+            arrived(c)
+            pressure_tile(c, 0)
+            return done
+
+        lax.fori_loop(0, tiles // 2, both_passes, 0)
+        lax.fori_loop(tiles // 2, tiles, pressure_pass, 0)
 
         def edges(columns, top_rows, bottom_rows):
             def level(k, packed):
@@ -319,26 +356,6 @@
         )
         start_all(ex_uv)
 
-        rho_s, rho_t = 0.5 * BETA_S, 0.5 * ALPHA_T
-        rho_0 = rho_t * T_REF - rho_s * S_REF
-
-        def pressure_tile(c, _):
-            k_cell = k_map[c, own, :]
-            scale = (TIME_STEP * GRAVITY) * (depth_map[c, own, :] / jnp.maximum(k_cell, 1.0))
-
-            def level(k, total):
-                half = (rho_s * sm[c, k, body_rows, :] - rho_t * tm[c, k, body_rows, :]) + rho_0
-                half = pick(real(k) < k_cell, half, zero)
-                middle = total + half
-                p[c, k, body_rows, :] = scale * middle
-                return middle + half
-
-            over_levels(level, zero)
-            return _
-
-        wait_all(tracer_load)
-        lax.fori_loop(0, tiles, pressure_tile, 0)
-
         (packed,) = edges((((0, p),),), ((p, fr_p),), ())
         cols_p[...] = packed
         ex_p = remote(sem_p, (fr_p, rn_p, SOUTH), (cols_p, east_p, WEST))
@@ -355,7 +372,7 @@
         far += corner_rims(pk_e2, pk_w2, rim_w2, rim_e2, baro_corners, HALO)
         start_all(far)
 
-        lax.fori_loop(0, tiles, tracer_tile, 0)
+        lax.fori_loop(tiles // 2, tiles, tracer_tile, 0)
         fr_t4, fr_s4 = split(first_row4)
         lr_t4, lr_s4, lr_v4 = split(last_row4)
         rn_t4, rn_s4 = split(row_n4)
@@ -399,9 +416,8 @@
                 kv_map[c, here, :] = k_v
                 dzu_map[c, here, :] = dz_u
                 dzv_map[c, here, :] = dz_v
-                wet_map[c, here, :] = pick(k_cell[c] > 0, dt_sub, 0.0)
-                hu_map[c, here, :] = dt_sub * (k_u * dz_u)
-                hv_map[c, here, :] = dt_sub * (k_v * dz_v)
+                hu_map[c, here, :] = (dt_sub * dt_sub) * (k_u * dz_u)
+                hv_map[c, here, :] = (dt_sub * dt_sub) * (k_v * dz_v)
 
         def in_blocks(work, start, n, size=BLOCK):
             lax.fori_loop(0, n // size, lambda i, _: (work(pl.multiple_of(start + size * i, PAD), size), _)[1], 0)
@@ -494,7 +510,7 @@
                 vs[c, k, here, :] = vv - (scaled(quarter, push) + (p[c, k, north, :] - pp[c]))
             return _
 
-        over_levels(momentum, 0)
+        over_levels(momentum, 0, FLOW_UNROLL)
 
         nil = jnp.zeros((SOLVE_ROWS, LANES), F32)
         parts = rows // SOLVE_ROWS
@@ -597,9 +613,9 @@
 
         def start_fields(start, n):
             here = pl.ds(start, n)
-            for ref, count in ((eta_map, k_out), (tu_map, ku_map), (tv_map, kv_map)):
+            for ref, count, unit in ((eta_map, k_out, 1.0), (tu_map, ku_map, dt_sub), (tv_map, kv_map, dt_sub)):
                 for c in range(ring):
-                    ref[c, here, :] = pick(count[c, here, :] > 0, ref[c, here, :], 0.0)
+                    ref[c, here, :] = pick(count[c, here, :] > 0, scaled(unit, ref[c, here, :]), 0.0)
 
         in_blocks(start_fields, PAD, full_n)
         tide_load.wait()
@@ -611,7 +627,7 @@
             here = pl.ds(start, n)
             for ref, count in ((fu_map, ku_map), (fv_map, kv_map)):
                 for c in range(ring):
-                    ref[c, here, :] = pick(count[c, here, :] > 0, dt_sub * ref[c, here, :], 0.0)
+                    ref[c, here, :] = pick(count[c, here, :] > 0, (dt_sub * dt_sub) * ref[c, here, :], 0.0)
 
         in_blocks(force_fields, PAD, full_n)
 
@@ -620,14 +636,14 @@
 
             def body(n, _):
                 tide_u, tide_v = tide[0, n], tide[1, n]
-                weight = weight_norm * ((n + 1) * (n_sub - n)).astype(F32)
+                weight = (weight_norm / dt_sub) * ((n + 1) * (n_sub - n)).astype(F32)
                 for r, n_r in chunks:
                     here, south = pl.ds(r, n_r), pl.ds(r - 1, n_r)
                     tu = [tu_map[c, here, :] for c in range(ring)]
                     tu_west = west(tu)
                     for c in range(ring):
                         spread = (tu[c] - tu_west[c]) + (tv_map[c, here, :] - tv_map[c, south, :])
-                        eta_map[c, here, :] = eta_map[c, here, :] - wet_map[c, here, :] * spread
+                        eta_map[c, here, :] = eta_map[c, here, :] - spread
                 for r, n_r in chunks:
                     here, north = pl.ds(r, n_r), pl.ds(r + 1, n_r)
                     eta = [eta_map[c, here, :] for c in range(ring)]
@@ -656,9 +672,9 @@
                 begin = end
             margin += PAD
 
-        for ref, out in zip((eta_map, tu_map, tv_map), split(baro_out)):
+        for ref, out, unit in zip((eta_map, tu_map, tv_map), split(baro_out), (1.0, 1.0 / dt_sub, 1.0 / dt_sub)):
             for c in range(tiles):
-                out[c] = ref[c, own, :]
+                out[c] = scaled(unit, ref[c, own, :])
 
         wait_all(ex_star)
         fill(((us, 0, west_us, None),), (), ((vs, rs_v4, None),))
@@ -699,24 +715,21 @@
                     vv = half * vv
                     for ref, store in zip((tm, sm), fluxes):
                         store[c, here, :] = vv * (ref[c, k, here, :] + ref[c, k, north, :])
-            for r in range(PAD, PAD + rows, BACK_ROWS):
-                here, south = pl.ds(r, BACK_ROWS), pl.ds(r - 1, BACK_ROWS)
-                flat = pl.ds(r - PAD + core, BACK_ROWS)
-                out_rows = pl.ds(r - PAD, BACK_ROWS)
-                uu = []
-                for c in range(ring):
-                    x = pick(kf < ku_map[c, flat, :], us[c, k, here, :] + cu_map[c, flat, :], 0.0)
-                    if c < tiles:
-                        u_o[i, out_rows, pl.ds(c * LANES, LANES)] = x
-                    uu.append(half * x)
-                for ref, store, out in zip((tm, sm), fluxes, (t_o, s_o)):
-                    tt = [ref[c, k, here, :] for c in range(ring)]
-                    fx = [x * (y + z) for x, y, z in zip(uu, tt, east(tt))]
-                    fx_west = west(fx)
-                    for c in range(tiles):
-                        spread = (fx[c] - fx_west[c]) + (store[c, here, :] - store[c, south, :])
-                        new = pick(kf < k_map[c, flat, :], tt[c] - spread, 0.0)
-                        out[i, out_rows, pl.ds(c * LANES, LANES)] = new
+            here, south, flat = body_rows, pl.ds(PAD - 1, rows), own
+            tracers = [[ref[c, k, here, :] for c in range(ring)] for ref in (tm, sm)]
+            easts = [east(x) for x in tracers]
+            uu = []
+            for c in range(ring):
+                x = pick(kf < ku_map[c, flat, :], us[c, k, here, :] + cu_map[c, flat, :], 0.0)
+                if c < tiles:
+                    u_o[i, :, pl.ds(c * LANES, LANES)] = x
+                uu.append(half * x)
+            fluxes_x = [[x * (y + z) for x, y, z in zip(uu, own_t, east_t)] for own_t, east_t in zip(tracers, easts)]
+            wests = [west(x) for x in fluxes_x]
+            for own_t, fx, fx_west, store, out in zip(tracers, fluxes_x, wests, fluxes, (t_o, s_o)):
+                for c in range(tiles):
+                    spread = (fx[c] - fx_west[c]) + (store[c, here, :] - store[c, south, :])
+                    out[i, :, pl.ds(c * LANES, LANES)] = pick(kf < k_map[c, flat, :], own_t[c] - spread, 0.0)
             return _
 
         lax.fori_loop(0, group, level, 0)
@@ -743,7 +756,7 @@
         scratch_shapes=[
             cube_buf, cube_buf, cube_buf, gain_buf, vmem(levels, SOLVE_ROWS, LANES),
             vmem(ring, ext_rows, LANES), pltpu.VMEM((tiles, rows, LANES), jnp.int32),
-            flat(2), flat(3), flat(3), flat(2), flat(3), flat(2), flat(2),
+            flat(2), flat(3), flat(3), flat(2), flat(2), flat(2), flat(2),
             pack_buf, pack_buf, rim_buf, rim_buf,
             vmem(4, rows, LANES), pack_buf, pack_buf, vmem(2, rows, LANES), line(3), line(2),
             line(3), line(2), corner_buf, corner_buf, line(2), line(3), line(2), line(3),

time: 66.9 us -> 66.1 us (0.988)
  Pallas kernels: 66.1 us -> 65.3 us
    pallas_call x1, Pallas kernels: 12.8 us -> 12 us  [local_step(): return tuple(back_call(*shared))]
where the time goes in v5:
time: 66.1 us; the launch traced here: 65.9 us
  Pallas kernels  65.3 us (99%)
    pallas_call x1, Pallas kernels, local_step(): front_call(vel_u, vel_v, temperature, salinity, sea_level, trans_u, trans...  53.3 us
    pallas_call x1, Pallas kernels, local_step(): return tuple(back_call(*shared))  12 us

profile of v5, /device:TPU:0, one launch (start us, length us, event | category | flops | bytes accessed | tf_op | source)
XLA Modules:
  0.0 65.9 jit_solution(14413096100233907959)
XLA Ops:
  0.6 53.3 %front.1 = (f32[5,31,80,128]{3,2,1,0:T(8,128)S(1)}, f32[4,31,80,128]{3,2,1,0:T(8,128)S(1)}, f32[5,31,80,128]{3,2,1,0:T(8,128)S(1)}, f32[5,31,80,128]{3,2,1,0:T(8...) custom-call(f32[31,64,512]{2,1,0:T(8,128)} %u_hbm.1, ...), custom_call_target="tpu_custom_call" | custom-call | tf_op jit(solution)/shard_map/front/pallas_call | solution.py:792
  53.9 12.0 %back.1 = (f32[64,512]{1,0:T(8,128)}, f32[64,512]{1,0:T(8,128)}, f32[64,512]{1,0:T(8,128)}, f32[31,64,512]{2,1,0:T(8,128)}, f32[31,64,512]{2,1,0:T(8,128)}, /*in...) custom-call(f32[5,31,80,128]{3,2,1,0:T(8,128)S(1)} %get-tuple-element.14.us, f32[4,31,80,128]{3,2,1,0:T(8,128)S(1)} %get-tuple-element.15.vs, ...), custom_call_target="tpu_custom_call" | custom-call | tf_op jit(solution)/shard_map/back/pallas_call | solution.py:795

commit v6 on v5

--- a/solution.py
+++ b/solution.py
@@ -237,12 +237,6 @@
         for c in range(tiles):
             k_map[c, own, :] = kmt_int[c].astype(F32)
         rim_pack((k_map, depth_map), pk_e1, pk_w1)
-        pl.semaphore_wait(barrier, len(COMPASS))
-        near_rows, near_cols, near_corners = split(sem_near)
-        near = row_rims(geo, near_rows, NEAR)
-        near += column_rims(pk_e1, pk_w1, rim_w1, rim_e1, near_cols)
-        near += corner_rims(pk_e1, pk_w1, rim_w1, rim_e1, near_corners, NEAR)
-        start_all(near)
 
         rho_s, rho_t = 0.5 * BETA_S, 0.5 * ALPHA_T
         rho_0 = rho_t * T_REF - rho_s * S_REF
@@ -314,6 +308,13 @@
 
         lax.fori_loop(0, tiles // 2, both_passes, 0)
         lax.fori_loop(tiles // 2, tiles, pressure_pass, 0)
+
+        pl.semaphore_wait(barrier, len(COMPASS))
+        near_rows, near_cols, near_corners = split(sem_near)
+        near = row_rims(geo, near_rows, NEAR)
+        near += column_rims(pk_e1, pk_w1, rim_w1, rim_e1, near_cols)
+        near += corner_rims(pk_e1, pk_w1, rim_w1, rim_e1, near_corners, NEAR)
+        start_all(near)
 
         def edges(columns, top_rows, bottom_rows):
             def level(k, packed):

time: 66.1 us -> 63.4 us (0.959)
  Pallas kernels: 65.3 us -> 62.6 us
    pallas_call x1, Pallas kernels: 53.3 us -> 50.6 us  [local_step(): front_call(vel_u, vel_v, temperature, salinity, sea_level, trans_u, trans...]
where the time goes in v6:
time: 63.4 us; the launch traced here: 63.2 us
  Pallas kernels  62.6 us (99%)
  between operations  0.64 us (1%)
    pallas_call x1, Pallas kernels, local_step(): front_call(vel_u, vel_v, temperature, salinity, sea_level, trans_u, trans...  50.6 us
    pallas_call x1, Pallas kernels, local_step(): return tuple(back_call(*shared))  12 us

profile of v6, /device:TPU:0, one launch (start us, length us, event | category | flops | bytes accessed | tf_op | source)
XLA Modules:
  0.0 63.2 jit_solution(998272676530371472)
XLA Ops:
  0.6 50.6 %front.1 = (f32[5,31,80,128]{3,2,1,0:T(8,128)S(1)}, f32[4,31,80,128]{3,2,1,0:T(8,128)S(1)}, f32[5,31,80,128]{3,2,1,0:T(8,128)S(1)}, f32[5,31,80,128]{3,2,1,0:T(8...) custom-call(f32[31,64,512]{2,1,0:T(8,128)} %u_hbm.1, ...), custom_call_target="tpu_custom_call" | custom-call | tf_op jit(solution)/shard_map/front/pallas_call | solution.py:793
  51.2 12.0 %back.1 = (f32[64,512]{1,0:T(8,128)}, f32[64,512]{1,0:T(8,128)}, f32[64,512]{1,0:T(8,128)}, f32[31,64,512]{2,1,0:T(8,128)}, f32[31,64,512]{2,1,0:T(8,128)}, /*in...) custom-call(f32[5,31,80,128]{3,2,1,0:T(8,128)S(1)} %get-tuple-element.14.us, f32[4,31,80,128]{3,2,1,0:T(8,128)S(1)} %get-tuple-element.15.vs, ...), custom_call_target="tpu_custom_call" | custom-call | tf_op jit(solution)/shard_map/back/pallas_call | solution.py:796

commit v7 on v6

--- a/solution.py
+++ b/solution.py
@@ -27,8 +27,8 @@
 SOLVE_ROWS = 32
 SUB_ROWS = 32
 UNROLL = 2
-EDGE_UNROLL = 3
-FLOW_UNROLL = 4
+EDGE_UNROLL = 5
+FLOW_UNROLL = 3
 MIB = 2**20
 
 
@@ -704,7 +704,7 @@
         half = 0.5 * TIME_STEP
 
         def level(i, _):
-            k = jnp.minimum(pl.program_id(0) * group + i, levels - 1)
+            k = pl.program_id(0) * group + i
             kf = k.astype(F32)
             for r in range(0, PAD + rows, PAD):
                 here, north = pl.ds(r, PAD), pl.ds(r + 1, PAD)
@@ -733,7 +733,8 @@
                     out[i, :, pl.ds(c * LANES, LANES)] = pick(kf < k_map[c, flat, :], own_t[c] - spread, 0.0)
             return _
 
-        lax.fori_loop(0, group, level, 0)
+        left = jnp.minimum(group, levels - pl.program_id(0) * group)
+        lax.fori_loop(0, left, level, 0)
 
     vmem = lambda *shape: pltpu.VMEM(shape, F32)
     flat = lambda n: vmem(n, ring, flat_rows, LANES)

time: 63.4 us -> 62.7 us (0.989)
  Pallas kernels: 62.6 us -> 61.9 us
where the time goes in v7:
time: 62.7 us; the launch traced here: 62.6 us
  Pallas kernels  61.9 us (99%)
  between operations  0.64 us (1%)
    pallas_call x1, Pallas kernels, local_step(): front_call(vel_u, vel_v, temperature, salinity, sea_level, trans_u, trans...  50.3 us
    pallas_call x1, Pallas kernels, local_step(): return tuple(back_call(*shared))  11.7 us

profile of v7, /device:TPU:0, one launch (start us, length us, event | category | flops | bytes accessed | tf_op | source)
XLA Modules:
  0.0 62.6 jit_solution(4053511762937270469)
XLA Ops:
  0.6 50.3 %front.1 = (f32[5,31,80,128]{3,2,1,0:T(8,128)S(1)}, f32[4,31,80,128]{3,2,1,0:T(8,128)S(1)}, f32[5,31,80,128]{3,2,1,0:T(8,128)S(1)}, f32[5,31,80,128]{3,2,1,0:T(8...) custom-call(f32[31,64,512]{2,1,0:T(8,128)} %u_hbm.1, ...), custom_call_target="tpu_custom_call" | custom-call | tf_op jit(solution)/shard_map/front/pallas_call | solution.py:794
  50.9 11.7 %back.1 = (f32[64,512]{1,0:T(8,128)}, f32[64,512]{1,0:T(8,128)}, f32[64,512]{1,0:T(8,128)}, f32[31,64,512]{2,1,0:T(8,128)}, f32[31,64,512]{2,1,0:T(8,128)}, /*in...) custom-call(f32[5,31,80,128]{3,2,1,0:T(8,128)S(1)} %get-tuple-element.14.us, f32[4,31,80,128]{3,2,1,0:T(8,128)S(1)} %get-tuple-element.15.vs, ...), custom_call_target="tpu_custom_call" | custom-call | tf_op jit(solution)/shard_map/back/pallas_call | solution.py:797
